TPU v7x, 32 devices: a whole 2x2x4 slice. The times are simulated.
32 devices in a mesh: ka: 4 (over y, x), ga: 8 (over z, core).
Axes of the slice: x: 2, y: 2, z: 4, core: 2. Of those that a mesh axis runs over, the one named last changes fastest.
Arguments:
- coeffs: bfloat16 [4, 1, 65536, 2, 512], P('ka', None, 'ga'), may hold values from -0.5 to 0.5
- counts: int32 [4, 1], replicated, may hold values from 32768 to 65536
- block_map: int32 [4, 1, 2048], replicated, may hold values from 0 to 2047, as said below
- wrap: int32 [4, 1, 2048], replicated, may hold values from 0 to 31
Outputs:
- margins: float32 [4, 512, 1, 2, 512], P('ka', 'ga')
Inputs may be any that keep to these rules, and one draw needn't show every extreme that they name: For each k-point and line, block_map is a permutation of the 2048 blocks. Counting G-shards as runs of 256 blocks, at most 33 blocks of one shard have their partner blocks in any one shard, and for each k-point and line some pair of shards reaches 33.
All inputs are finite; a program needn't handle non-finite values.
Results may differ from a plain program's by a relative error of at most 0.0003.
Values may be sent and summed in bfloat16 or wider, within the bound.
No kernel may reach another device: no remote copies, remote signals or barrier semaphores. Data moves between devices by JAX's collectives and lax.ppermute only.
A program may use at most 128 MiB of HBM per device.

v0:
```python
import jax
import jax.numpy as jnp
from jax import lax
from jax.sharding import PartitionSpec as P

BLK = 32


def from_behind(value, axis, steps):
    count = lax.axis_size(axis)
    pairs = [(source, (source + steps) % count) for source in range(count)]
    return lax.ppermute(value, axis, pairs)


def slot_table(dest, ranking, values, shard_count, capacity):
    shard_ids = jnp.arange(shard_count, dtype=jnp.int32)
    slot_ids = jnp.arange(capacity, dtype=jnp.int32)
    hit = (dest[:, :, None, None] == shard_ids[None, None, :, None]) & (
        ranking[:, :, None, None] == slot_ids[None, None, None, :]
    )
    return jnp.sum(jnp.where(hit, values[:, :, None, None], 0), axis=1)


def pick_rows(source, picks):
    return jax.vmap(lambda rows_in, index_in: jnp.take(rows_in, index_in, axis=0))(source, picks)


def local(coeffs, counts, block_map, wrap):
    held_k = coeffs[0]
    line_count, g_rows, _, band_count = held_k.shape
    shard_count = lax.axis_size("ga")
    per_shard = g_rows // BLK
    block_total = block_map.shape[-1]
    capacity = block_total // (shard_count * shard_count) + 1
    k_index = lax.axis_index("ka")
    g_index = lax.axis_index("ga")
    k_total = counts.shape[0]
    count_here = counts[k_index]
    count_next = counts[(k_index + 1) % k_total]
    block_src = block_map[k_index]
    wrap_src = wrap[k_index]
    lane_ids = jnp.arange(BLK, dtype=jnp.int32)
    block_mine = lax.dynamic_slice_in_dim(block_src, g_index * per_shard, per_shard, 1)
    wrap_mine = lax.dynamic_slice_in_dim(wrap_src, g_index * per_shard, per_shard, 1)
    lane_shift = (lane_ids[None, None, :] + wrap_mine[:, :, None]) % BLK
    src_rows = block_mine[:, :, None] * BLK + lane_shift
    own_rows = g_index * g_rows + jnp.arange(g_rows, dtype=jnp.int32).reshape(per_shard, BLK)
    usable = (own_rows[None] < count_here[:, None, None]) & (src_rows < count_next[:, None, None])
    usable = usable.reshape(line_count, g_rows)
    masked_k = jnp.where(usable[:, :, None, None], held_k, jnp.zeros((), held_k.dtype))
    source_dev = block_mine // per_shard
    same_dev = source_dev[:, :, None] == source_dev[:, None, :]
    earlier = jnp.arange(per_shard)[:, None] > jnp.arange(per_shard)[None, :]
    rank_mine = jnp.sum((same_dev & earlier[None]).astype(jnp.int32), axis=2)
    coming = from_behind(held_k, "ka", -1)
    blocks_held = masked_k.reshape(line_count, per_shard, BLK, 2, band_count)
    back_lanes = (lane_ids[None, None, :] - wrap_mine[:, :, None]) % BLK
    rotated = jax.vmap(jax.vmap(lambda rows_in, index_in: jnp.take(rows_in, index_in, axis=0)))(
        blocks_held, back_lanes
    )
    local_ids = jnp.arange(per_shard, dtype=jnp.int32)[None, :]
    send_table = slot_table(source_dev, rank_mine, local_ids, shard_count, capacity)
    outgoing = pick_rows(rotated, send_table.reshape(line_count, -1))
    outgoing = outgoing.reshape(line_count, shard_count, capacity * BLK, 2, band_count)
    incoming = lax.all_to_all(outgoing, "ga", split_axis=1, concat_axis=1, tiled=True)
    incoming = incoming.reshape(line_count, shard_count * capacity * BLK, 2, band_count)
    inverse = jax.vmap(
        lambda perm_in: jnp.zeros((block_total,), jnp.int32)
        .at[perm_in]
        .set(jnp.arange(block_total, dtype=jnp.int32))
    )(block_src)
    target_mine = lax.dynamic_slice_in_dim(inverse, g_index * per_shard, per_shard, 1)
    sender = target_mine // per_shard
    to_me = block_src // per_shard == g_index
    rank_to_me = (
        jnp.cumsum(to_me.reshape(line_count, shard_count, per_shard).astype(jnp.int32), axis=2) - 1
    ).reshape(line_count, block_total)
    rank_sent = jnp.take_along_axis(rank_to_me, target_mine, axis=1)
    row_index = (
        (sender * capacity + rank_sent)[:, :, None] * BLK + lane_ids[None, None, :]
    ).reshape(line_count, g_rows)
    left_side = pick_rows(incoming, row_index)
    rows_here = band_count // shard_count
    products = jnp.einsum("lgcm,lgdn->mlcdn", left_side, coming, preferred_element_type=jnp.float32)
    real_part = products[:, :, 0, 0] + products[:, :, 1, 1]
    imag_part = products[:, :, 0, 1] - products[:, :, 1, 0]
    summed = lax.psum(jnp.stack([real_part, imag_part], axis=2), "ga")
    result = lax.dynamic_slice_in_dim(summed, g_index * rows_here, rows_here, 0)
    return result[None]


def solution(mesh):
    placed = (P("ka", None, "ga", None, None), P(), P(), P())
    return jax.shard_map(
        local,
        mesh=mesh,
        in_specs=placed,
        out_specs=P("ka", "ga", None, None, None),
        check_vma=False,
    )
```

profile of v0, /device:TPU:0, one launch (start us, length us, event | category | flops | bytes accessed | tf_op | source)
XLA Modules:
  0.0 826.9 jit_solution(5665315744447065316)
XLA Ops:
  6.5 0.8 and_select_fusion
  7.3 0.2 convert_reduce_fusion
  7.5 0.7 select_reduce_fusion
  8.6 0.1 broadcast_in_dim.90
  8.7 0.1 broadcast_in_dim.91
  9.0 1.4 constant_dynamic-slice_fusion.1
  10.4 1.6 compare_and_fusion
  12.0 21.3 %broadcast_select_fusion.2 = bf16[1,256,32,2,512]{4,3,2,1,0:T(2,128)(2,1)} fusion(bf16[1,256,32,2,512]{4,3,2,1,0:T(2,128)(2,1)} %bitcast.68, pred[256,32]{1,0:T(8,128)(4,1)S(1)} %get-tuple-element.14), kind=kLoop, calls=%fused_computation.7 | loop fusion | flops 8388608 | bytes 33562624 | tf_op jit(solution)/shard_map/jit(_where)/select_n | solution.py:50
  33.4 99.0 %gather_fusion.1 = bf16[8192,2,512]{2,1,0:T(2,128)(2,1)} fusion(bf16[1,256,32,2,512]{4,3,2,1,0:T(2,128)(2,1)} %broadcast_select_fusion.2, s32[8192]{0:T(1024)S(1)} %reshape.1065), kind=kCustom, calls=%fused_computation.1 | custom fusion | bytes 33652736 | tf_op jit(solution)/shard_map/vmap(vmap(jit(_take)))/gather | solution.py:58
  132.4 21.7 %broadcast_select_fusion.3 = bf16[1,256,32,2,512]{4,3,2,1,0:T(2,128)(2,1)} fusion(bf16[1,256,32,2,512]{4,3,2,1,0:T(2,128)(2,1)} %bitcast.69, pred[256,32]{1,0:T(8,128)(4,1)S(1)} %get-tuple-element.13), kind=kLoop, calls=%fused_computation.8 | loop fusion | flops 8388608 | bytes 33562624 | tf_op jit(solution)/shard_map/vmap(vmap(jit(_take)))/select_n | solution.py:58
  154.0 47.2 %gather_fusion.2 = bf16[264,32,2,512]{3,2,1,0:T(2,128)(2,1)} fusion(bf16[1,256,32,2,512]{4,3,2,1,0:T(2,128)(2,1)} %broadcast_select_fusion.3, s32[264]{0:T(512)S(1)} %fusion.45), kind=kCustom, calls=%fused_computation.2 | custom fusion | bytes 34605120 | tf_op jit(solution)/shard_map/vmap(jit(_take))/gather | solution.py:25
  201.2 25.0 %broadcast_select_fusion = bf16[1,8,1056,2,512]{4,3,2,0,1:T(2,128)(2,1)} fusion(bf16[1,8,1056,2,512]{4,3,2,0,1:T(2,128)(2,1)} %bitcast.67, pred[8,1056]{1,0:T(8,128)(4,1)S(1)} %broadcast_in_dim.91), kind=kLoop, calls=%fused_computation.5 | loop fusion | flops 8650752 | bytes 34611456 | tf_op jit(solution)/shard_map/vmap(jit(_take))/select_n | solution.py:25
  226.2 6.3 all-to-all-start
  232.7 15.8 %copy.58 = bf16[1,1,8192,2,512]{4,2,3,1,0:T(8,128)(2,1)} copy(bf16[1,1,8192,2,512]{4,3,2,1,0:T(2,128)(2,1)} %param.4) | data formatting | bytes 33554432 | tf_op args[0]
  248.5 3.4 collective-permute-start
  251.8 0.7 compare_select_fusion.5
  252.6 0.6 reduce-window.6
  253.2 0.2 slice_reduce_fusion
  253.5 0.1 and_reduce_fusion
  253.7 8.2 scatter_custom_fusion
  262.2 1.7 gather_fusion
  264.0 0.1 add.375
  264.3 0.1 add.377
  264.7 343.0 %all-to-all-done = bf16[1,8,1056,2,512]{4,3,2,0,1:T(2,128)(2,1)} async-done(((bf16[1,8,1056,2,512]{4,3,2,0,1:T(2,128)(2,1)}), bf16[1,8,1056,2,512]{4,3,2,0,1:T(2,128)(2,1)}, u32[]{:S(2)}, u32[]{:S(2)}) %all-to-all-start) | async-done | bytes 17301536 | tf_op jit(solution)/shard_map/all_to_all | solution.py:65
  607.8 91.4 %gather_fusion.3 = bf16[8192,2,512]{2,1,0:T(2,128)(2,1)} fusion(bf16[1,8448,2,512]{3,2,1,0:T(2,128)(2,1)} %bitcast.20, s32[8192]{0:T(1024)S(1)} %bitcast.65), kind=kCustom, calls=%fused_computation.3 | custom fusion | bytes 33619968 | tf_op jit(solution)/shard_map/vmap(jit(_take))/gather | solution.py:25
  699.2 31.5 %fusion.3 = bf16[8192,2,512,1]{2,1,0,3:T(2,128)(2,1)S(1)} fusion(bf16[8192,2,512]{2,1,0:T(2,128)(2,1)} %gather_fusion.3, pred[8192]{0:T(1024)(128)(4,1)S(1)} %compare_and_fusion.1), kind=kLoop, calls=%fused_computation.13 | loop fusion | flops 8388608 | bytes 33562624 | tf_op jit(solution)/shard_map/vmap(jit(_take))/select_n | solution.py:25
  730.7 20.7 %fusion.4 = f32[512,1,2,2,512]{4,0,3,2,1:T(8,128)S(1)} fusion(bf16[1,8192,2,512]{3,1,2,0:T(8,128)(2,1)} %collective-permute-done, bf16[8192,2,512,1]{2,1,0,3:T(2,128)(2,1)S(1)} %fusion.3), kind=kOutput, calls=%fused_computation.14 | convolution fusion | flops 17179869184 | bytes 37748736 | tf_op jit(solution)/shard_map/lgcm,lgdn->mlcdn/dot_general | solution.py:84
  751.4 0.5 fusion.10
  751.9 1.5 pad_maximum_fusion
  753.4 64.8 %all-reduce.2.cloned.1.call-done = f32[512,1,2,512]{3,0,2,1:T(8,128)} async-done(((f32[512,1,2,512]{3,0,2,1:T(8,128)}), f32[512,1,2,512]{3,0,2,1:T(8,128)}) %all-reduce.2.cloned.1.call-update) | async-done | bytes 2097168 | tf_op jit(solution)/shard_map/psum | solution.py:87
  818.2 1.0 dynamic-slice_bitcast_fusion
  819.1 0.9 copy.48
  (47 shorter events, 1.6 us)
Async XLA Ops:
  226.2 381.5 %all-to-all-start = ((bf16[1,8,1056,2,512]{4,3,2,0,1:T(2,128)(2,1)}), bf16[1,8,1056,2,512]{4,3,2,0,1:T(2,128)(2,1)}, u32[]{:S(2)}, u32[]{:S(2)}) async-start(bf16[1,8,1056,2,512]{4,3,2,0,1:T(2,128)(2,1)} %broadcast_select_fusion), calls=%async_computation | async-start | bytes 34603008 | tf_op jit(solution)/shard_map/all_to_all | solution.py:65
  232.6 20.8 %copy-start = (s32[2]{0:T(128)S(1)}, s32[2]{0:T(128)}, u32[]{:S(2)}) copy-start(s32[2]{0:T(128)} %constant.184) | copy-start | bytes 28
  232.6 20.9 %copy-start.1 = (s32[2]{0:T(128)S(1)}, s32[2]{0:T(128)}, u32[]{:S(2)}) copy-start(s32[2]{0:T(128)} %constant.187) | copy-start | bytes 28
  232.6 585.6 %all-reduce.2.cloned.1.call-start = ((), (), s32[]{:S(2)}) async-start(), calls=%async_computation.1 | async-start | bytes 4194304 | tf_op jit(solution)/shard_map/psum | solution.py:87
  248.5 482.2 %collective-permute-start = (bf16[1,8192,2,512]{3,1,2,0:T(8,128)(2,1)}, bf16[1,8192,2,512]{3,1,2,0:T(8,128)(2,1)}, u32[]{:S(2)}, u32[]{:S(2)}) collective-permute-start(bf16[1,8192,2,512]{3,1,2,0:T(8,128)(2,1)} %bitcast.63), channel_id=1, source_target_pairs={{0,24},{8,0},{16,8},{24,16},{1,25},{9,1},{17,9},{25,17},{2,26},{10... | collective-permute-start | bytes 50331656 | tf_op jit(solution)/shard_map/ppermute | solution.py:12
Sparse Core Ops, SparseCore 0:
  753.5 64.6 all-reduce.1
where the time goes:
time: 827 us
  waiting for transfers between devices  408 us (49%)
  local copies, waits for them, and re-layouts  268 us (32%)
  other arithmetic  107 us (13%)
  matrix products  20.7 us (3%)
  between operations  13.7 us (2%)
  starting transfers between devices  9.75 us (1%)
    all_to_all x1, waiting for transfers between devices, local(): lax.all_to_all(outgoing, 'ga', split_axis=1, concat_axis=1, tiled=True)  343 us
    gather x4, local copies, waits for them, and re-layouts, pick_rows(): jnp.take(rows_in, index_in, axis=0)  139 us
    gather x3, local copies, waits for them, and re-layouts, local(): jnp.take(rows_in, index_in, axis=0)  99.2 us
    psum x1, waiting for transfers between devices, local(): summed = lax.psum(jnp.stack([real_part, imag_part], axis=2), 'ga')  64.8 us
    select_n x4, other arithmetic, pick_rows(): jnp.take(rows_in, index_in, axis=0)  56.6 us
    unnamed x9, local copies, waits for them, and re-layouts  24.2 us
    select_n x2, other arithmetic, local(): jnp.take(rows_in, index_in, axis=0)  21.7 us
    select_n x1, other arithmetic, local(): jnp.where(usable[:, :, None, None], held_k, jnp.zeros((), held_k.dtype))  21.3 us
  transfers between devices with their start and end apart: 3, of which 2 were waited for; matrix products, arithmetic and copies ran while one was open for 18% of the time, Pallas kernels for 0%

commit v1 on v0

v1 whole, which is shorter than its diff:
```python
import functools

import jax
import jax.numpy as jnp
from jax import lax
from jax.experimental import pallas as pl
from jax.experimental.pallas import tpu as pltpu
from jax.sharding import PartitionSpec as P

BLK = 32


def chunk_bounds(capacity):
    pieces = 3 if capacity >= 3 else 1
    return [(capacity * i // pieces, capacity * (i + 1) // pieces) for i in range(pieces)]


def pack_kernel(first, capacity, group, rotate, table, *refs):
    ins, out = refs[:group], refs[group]
    slots = table.shape[0] // 4
    rank = first + pl.program_id(0)
    for d in range(group):
        entry = (pl.program_id(1) * group + d) * capacity + rank
        if not rotate:
            out[d, 0] = ins[d][...]
            continue
        shift = table[slots + entry]
        left_end = table[2 * slots + entry]
        right_end = table[3 * slots + entry]
        for p in range(BLK):
            lane = (p - shift) & (BLK - 1)
            row = ins[d][lane]
            live = (lane < left_end) & (p < right_end)
            out[d, 0, p] = jnp.where(live, row, jnp.zeros_like(row))


def pack(source, table, bounds, capacity, shards, rotate):
    first, last = bounds
    group = min(8, shards)
    _, _, bands = source.shape
    ranks = last - first

    def picked(d):
        return lambda r, s, table: (table[(s * group + d) * capacity + first + r], 0, 0)

    moved = shards * ranks * BLK * 2 * bands * 2
    return pl.pallas_call(
        functools.partial(pack_kernel, first, capacity, group, rotate),
        grid_spec=pltpu.PrefetchScalarGridSpec(
            num_scalar_prefetch=1,
            grid=(ranks, shards // group),
            in_specs=[pl.BlockSpec((BLK, 2, bands), picked(d)) for d in range(group)],
            out_specs=pl.BlockSpec((group, 1, BLK, 2, bands), lambda r, s, table: (s, r, 0, 0, 0)),
        ),
        out_shape=jax.ShapeDtypeStruct((shards, ranks, BLK, 2, bands), source.dtype),
        cost_estimate=pl.CostEstimate(flops=4 * moved, bytes_accessed=2 * moved, transcendentals=0),
        name="pack_left" if rotate else "pack_right",
    )(table, *([source] * group))


def local(coeffs, counts, block_map, wrap):
    held = coeffs[0]
    lines, g_rows, _, bands = held.shape
    shards = lax.axis_size("ga")
    per_shard = g_rows // BLK
    blocks = block_map.shape[-1]
    capacity = blocks // (shards * shards) + 1
    k_total = counts.shape[0]
    k = lax.axis_index("ka")
    g = lax.axis_index("ga")
    k_next = (k + 1) % k_total
    k_prev = (k + k_total - 1) % k_total
    ids = jnp.arange(per_shard, dtype=jnp.int32)
    slot_ids = jnp.arange(capacity, dtype=jnp.int32)
    shard_ids = jnp.arange(shards, dtype=jnp.int32)
    down = [(s, (s - 1) % k_total) for s in range(k_total)]
    rows_here = bands // shards
    outs = []
    for line in range(lines):
        mine = lax.dynamic_slice_in_dim(block_map[k, line], g * per_shard, per_shard, 0)
        shift = lax.dynamic_slice_in_dim(wrap[k, line], g * per_shard, per_shard, 0)
        target = mine // per_shard
        rank = jnp.sum(
            ((target[:, None] == target[None, :]) & (ids[:, None] > ids[None, :])).astype(jnp.int32), axis=1
        )
        left_end = counts[k, line] - (g * g_rows + ids * BLK)
        right_end = counts[k_next, line] - mine * BLK
        hit = (target[None, None, :] == shard_ids[:, None, None]) & (rank[None, None, :] == slot_ids[None, :, None])
        values = jnp.stack([ids, shift, left_end, right_end])
        left_table = jnp.sum(jnp.where(hit[None], values[:, None, None, :], 0), axis=3).reshape(-1)
        theirs = block_map[k_prev, line].reshape(shards, per_shard)
        for_me = theirs // per_shard == g
        rank_in = jnp.sum((for_me[:, None, :] & (ids[:, None] > ids[None, :])[None]).astype(jnp.int32), axis=2)
        hit_in = for_me[:, None, :] & (rank_in[:, None, :] == slot_ids[None, :, None])
        right_table = jnp.sum(jnp.where(hit_in, (theirs % per_shard)[:, None, :], 0), axis=2).reshape(-1)
        right_table = jnp.concatenate([right_table] * 4)

        rows = held[line]
        total = None
        for bounds in chunk_bounds(capacity):
            sent = pack(rows, left_table, bounds, capacity, shards, True)
            left = lax.all_to_all(sent, "ga", split_axis=0, concat_axis=0, tiled=True)
            right = pack(rows, right_table, bounds, capacity, shards, False)
            right = lax.ppermute(right, "ka", down)
            count = shards * (bounds[1] - bounds[0]) * BLK
            products = jnp.einsum(
                "gcm,gdn->mcdn",
                left.reshape(count, 2, bands),
                right.reshape(count, 2, bands),
                preferred_element_type=jnp.float32,
            )
            part = jnp.stack(
                [products[:, 0, 0] + products[:, 1, 1], products[:, 0, 1] - products[:, 1, 0]], axis=1
            )
            total = part if total is None else total + part
        outs.append(lax.psum_scatter(total, "ga", scatter_dimension=0, tiled=True))
    return jnp.stack(outs, axis=1)[None]


def solution(mesh):
    placed = (P("ka", None, "ga", None, None), P(), P(), P())
    return jax.shard_map(
        local,
        mesh=mesh,
        in_specs=placed,
        out_specs=P("ka", "ga", None, None, None),
        check_vma=False,
    )
```

time: 827 us -> 647 us (0.78)
  local copies, waits for them, and re-layouts: 268 us -> 9.76 us
  other arithmetic: 107 us -> 10.9 us
  waiting for transfers between devices: 408 us -> 492 us
  Pallas kernels: 0 us -> 65.4 us
  starting transfers between devices: 9.75 us -> 20.4 us
  matrix products: 20.7 us -> 29.8 us
    gather x8 -> x0, local copies, waits for them, and re-layouts: 240 us -> none  [the longest x4 139 us: pick_rows(): jnp.take(rows_in, index_in, axis=0)]
    ppermute x1 -> x3, waiting for transfers between devices: 0.01 us -> 230 us  [local(): right = lax.ppermute(right, 'ka', down)]
    all_to_all x1 -> x3, waiting for transfers between devices: 343 us -> 196 us  [local(): left = lax.all_to_all(sent, 'ga', split_axis=0, concat_axis=0, tiled=True)]
    select_n x11 -> x3, other arithmetic: 101 us -> 0.78 us  [the longest x2 0.77 us: local(): target = mine // per_shard]
    unnamed x1 -> x2, waiting for transfers between devices: 0.02 us -> 66 us
    pallas_call x0 -> x6, Pallas kernels: none -> 65.4 us  [pack(): pl.pallas_call(functools.partial(pack_kernel, first, capacity, group, rot...]
    psum x1 -> x0, waiting for transfers between devices: 64.8 us -> none  [local(): summed = lax.psum(jnp.stack([real_part, imag_part], axis=2), 'ga')]
    unnamed x9, local copies, waits for them, and re-layouts: 24.2 us -> 1.94 us
  transfers between devices with their start and end apart: 3 -> 7, of which waited for: 2 -> 6; matrix products, arithmetic and copies ran while one was open for 18% -> 4% of each run, Pallas kernels for 0% -> 8%
where the time goes in v1:
time: 647 us; the launch traced here: 642 us
  waiting for transfers between devices  492 us (76%)
  Pallas kernels  65.4 us (10%)
  matrix products  29.8 us (5%)
  starting transfers between devices  20.4 us (3%)
  between operations  14.3 us (2%)
  other arithmetic  10.9 us (2%)
  local copies, waits for them, and re-layouts  9.76 us (2%)
    ppermute x3, waiting for transfers between devices, local(): right = lax.ppermute(right, 'ka', down)  230 us
    all_to_all x3, waiting for transfers between devices, local(): left = lax.all_to_all(sent, 'ga', split_axis=0, concat_axis=0, tiled=True)  196 us
    unnamed x2, waiting for transfers between devices  66 us
    pallas_call x6, Pallas kernels, pack(): pl.pallas_call(functools.partial(pack_kernel, first, capacity, group, rot...  65.4 us
    dot_general x3, matrix products, local(): jnp.einsum('gcm,gdn->mcdn', left.reshape(count, 2, bands), right.reshape(...  29.8 us
    all_to_all x3, starting transfers between devices, local(): left = lax.all_to_all(sent, 'ga', split_axis=0, concat_axis=0, tiled=True)  15.7 us
  transfers between devices with their start and end apart: 7, of which 6 were waited for; matrix products, arithmetic and copies ran while one was open for 4% of the time, Pallas kernels for 8%

profile of v1, /device:TPU:0, one launch (start us, length us, event | category | flops | bytes accessed | tf_op | source)
XLA Modules:
  0.0 642.3 jit_solution(7084806037086598135)
XLA Ops:
  6.5 0.8 and_select_fusion
  7.5 1.4 constant_dynamic-slice_fusion.1
  8.9 1.4 fusion.39
  11.0 2.3 select_reduce_fusion
  13.4 0.7 reshape.320.table
  14.1 12.7 %pack_left.3 = bf16[8,11,32,2,512]{4,3,2,1,0:T(2,128)(2,1)} custom-call(s32[1056]{0:T(1024)} %reshape.320.table, bf16[8192,2,512]{2,1,0:T(2,128)(2,1)} %bitcast.68, bf16[8192,2,512]{2,1,0:T(2,128)(2,1)} %bitcast.69, bf16[8192,2,512]{2,1,0:T(2,128)(2,1)} %bitcast.70, bf16[8192,2,512]{2,1,0:T(2,128)(2,1)} %bitcast.71, bf16[8192,2,512]{2,1,0:T(2,128)(2,1)} %bitcast.72, ...), custom_call_target="tpu_custom_call" | custom-call | flops 23068672 | bytes 11534336 | tf_op jit(solution)/shard_map/pack_left/pallas_call | solution.py:47
  26.8 6.4 all-to-all-start
  33.1 12.6 %pack_left.4 = bf16[8,11,32,2,512]{4,3,2,1,0:T(2,128)(2,1)} custom-call(s32[1056]{0:T(1024)} %reshape.320.table, bf16[8192,2,512]{2,1,0:T(2,128)(2,1)} %bitcast.76, bf16[8192,2,512]{2,1,0:T(2,128)(2,1)} %bitcast.77, bf16[8192,2,512]{2,1,0:T(2,128)(2,1)} %bitcast.78, bf16[8192,2,512]{2,1,0:T(2,128)(2,1)} %bitcast.79, bf16[8192,2,512]{2,1,0:T(2,128)(2,1)} %bitcast.80, ...), custom_call_target="tpu_custom_call" | custom-call | flops 23068672 | bytes 11534336 | tf_op jit(solution)/shard_map/pack_left/pallas_call | solution.py:47
  45.8 115.1 %all-to-all-done = bf16[8,11,32,2,512]{4,3,2,1,0:T(2,128)(2,1)} async-done(((bf16[8,11,32,2,512]{4,3,2,1,0:T(2,128)(2,1)}), bf16[8,11,32,2,512]{4,3,2,1,0:T(2,128)(2,1)}, u32[]{:S(2)}, u32[]{:S(2)}) %all-to-all-start) | async-done | bytes 5767200 | tf_op jit(solution)/shard_map/all_to_all | solution.py:102
  160.9 4.7 all-to-all-start.1
  165.6 0.7 dynamic-slice_reduce_fusion
  168.3 9.2 %pack_right.3 = bf16[8,11,32,2,512]{4,3,2,1,0:T(2,128)(2,1)} custom-call(s32[1056]{0:T(1024)} %concatenate.3.table, bf16[8192,2,512]{2,1,0:T(2,128)(2,1)} %bitcast.91, bf16[8192,2,512]{2,1,0:T(2,128)(2,1)} %bitcast.85, bf16[8192,2,512]{2,1,0:T(2,128)(2,1)} %bitcast.86, bf16[8192,2,512]{2,1,0:T(2,128)(2,1)} %bitcast.87, bf16[8192,2,512]{2,1,0:T(2,128)(2,1)} %bitcast.88, ...), custom_call_target="tpu_custom_call" | custom-call | flops 23068672 | bytes 11534336 | tf_op jit(solution)/shard_map/pack_right/pallas_call | solution.py:47
  177.5 2.4 collective-permute-start
  179.9 9.2 %pack_right.4 = bf16[8,11,32,2,512]{4,3,2,1,0:T(2,128)(2,1)} custom-call(s32[1056]{0:T(1024)} %concatenate.3.table, bf16[8192,2,512]{2,1,0:T(2,128)(2,1)} %bitcast.92, bf16[8192,2,512]{2,1,0:T(2,128)(2,1)} %bitcast.93, bf16[8192,2,512]{2,1,0:T(2,128)(2,1)} %bitcast.94, bf16[8192,2,512]{2,1,0:T(2,128)(2,1)} %bitcast.95, bf16[8192,2,512]{2,1,0:T(2,128)(2,1)} %bitcast.96, ...), custom_call_target="tpu_custom_call" | custom-call | flops 23068672 | bytes 11534336 | tf_op jit(solution)/shard_map/pack_right/pallas_call | solution.py:47
  189.6 9.2 %pack_right.5 = bf16[8,11,32,2,512]{4,3,2,1,0:T(2,128)(2,1)} custom-call(s32[1056]{0:T(1024)} %concatenate.3.table, bf16[8192,2,512]{2,1,0:T(2,128)(2,1)} %bitcast.100, bf16[8192,2,512]{2,1,0:T(2,128)(2,1)} %bitcast.101, bf16[8192,2,512]{2,1,0:T(2,128)(2,1)} %bitcast.102, bf16[8192,2,512]{2,1,0:T(2,128)(2,1)} %bitcast.103, bf16[8192,2,512]{2,1,0:T(2,128)(2,1)} %bitcast.104, ...), custom_call_target="tpu_custom_call" | custom-call | flops 23068672 | bytes 11534336 | tf_op jit(solution)/shard_map/pack_right/pallas_call | solution.py:47
  198.8 1.4 collective-permute-start.2
  200.2 12.6 %pack_left.5 = bf16[8,11,32,2,512]{4,3,2,1,0:T(2,128)(2,1)} custom-call(s32[1056]{0:T(1024)} %reshape.320.table, bf16[8192,2,512]{2,1,0:T(2,128)(2,1)} %bitcast.108, bf16[8192,2,512]{2,1,0:T(2,128)(2,1)} %bitcast.109, bf16[8192,2,512]{2,1,0:T(2,128)(2,1)} %bitcast.110, bf16[8192,2,512]{2,1,0:T(2,128)(2,1)} %bitcast.111, bf16[8192,2,512]{2,1,0:T(2,128)(2,1)} %bitcast.112, ...), custom_call_target="tpu_custom_call" | custom-call | flops 23068672 | bytes 11534336 | tf_op jit(solution)/shard_map/pack_left/pallas_call | solution.py:47
  212.8 80.5 %all-to-all-done.1 = bf16[8,11,32,2,512]{4,3,2,1,0:T(2,128)(2,1)} async-done(((bf16[8,11,32,2,512]{4,3,2,1,0:T(2,128)(2,1)}), bf16[8,11,32,2,512]{4,3,2,1,0:T(2,128)(2,1)}, u32[]{:S(2)}, u32[]{:S(2)}) %all-to-all-start.1) | async-done | bytes 5767200 | tf_op jit(solution)/shard_map/all_to_all | solution.py:102
  293.3 4.7 all-to-all-start.2
  298.2 6.7 %collective-permute-done = bf16[8,11,32,2,512]{4,3,2,1,0:T(2,128)(2,1)} collective-permute-done((bf16[8,11,32,2,512]{4,3,2,1,0:T(2,128)(2,1)}, bf16[8,11,32,2,512]{4,3,2,1,0:T(2,128)(2,1)}, u32[]{:S(2)}, u32[]{:S(2)}) %collective-permute-start) | collective-permute-done | bytes 5767200 | tf_op jit(solution)/shard_map/ppermute | solution.py:104
  304.9 10.0 %fusion.12 = f32[512,2,2,512]{0,3,1,2:T(8,128)S(1)} fusion(bf16[8,11,32,2,512]{4,3,2,1,0:T(2,128)(2,1)} %all-to-all-done, bf16[8,11,32,2,512,1]{4,3,2,1,0,5:T(2,128)(2,1)} %bitcast.1), kind=kOutput, calls=%fused_computation.12 | convolution fusion | flops 5905580032 | bytes 15728640 | tf_op jit(solution)/shard_map/gcm,gdn->mcdn/dot_general | solution.py:106
  315.1 1.2 fusion.34
  316.3 112.2 %collective-permute-done.1 = bf16[8,11,32,2,512]{4,3,2,1,0:T(2,128)(2,1)} collective-permute-done((bf16[8,11,32,2,512]{4,3,2,1,0:T(2,128)(2,1)}, bf16[8,11,32,2,512]{4,3,2,1,0:T(2,128)(2,1)}, u32[]{:S(2)}, u32[]{:S(2)}) %collective-permute-start.1) | collective-permute-done | bytes 5767200 | tf_op jit(solution)/shard_map/ppermute | solution.py:104
  428.5 9.9 %fusion.17 = f32[512,2,2,512]{0,3,2,1:T(8,128)S(1)} fusion(bf16[8,11,32,2,512,1]{4,3,2,1,0,5:T(2,128)(2,1)} %bitcast.17, bf16[8,11,32,2,512]{4,3,2,1,0:T(2,128)(2,1)} %collective-permute-done.1), kind=kOutput, calls=%fused_computation.13 | convolution fusion | flops 5905580032 | bytes 15728640 | tf_op jit(solution)/shard_map/gcm,gdn->mcdn/dot_general | solution.py:106
  438.4 1.9 fusion.31
  440.3 111.2 %collective-permute-done.2 = bf16[8,11,32,2,512]{4,3,2,1,0:T(2,128)(2,1)} collective-permute-done((bf16[8,11,32,2,512]{4,3,2,1,0:T(2,128)(2,1)}, bf16[8,11,32,2,512]{4,3,2,1,0:T(2,128)(2,1)}, u32[]{:S(2)}, u32[]{:S(2)}) %collective-permute-start.2) | collective-permute-done | bytes 5767200 | tf_op jit(solution)/shard_map/ppermute | solution.py:104
  551.5 9.9 %fusion.22 = f32[512,2,2,512]{0,3,2,1:T(8,128)S(1)} fusion(bf16[8,11,32,2,512,1]{4,3,2,1,0,5:T(2,128)(2,1)} %bitcast.24, bf16[8,11,32,2,512]{4,3,2,1,0:T(2,128)(2,1)} %collective-permute-done.2), kind=kOutput, calls=%fused_computation.14 | convolution fusion | flops 5905580032 | bytes 15728640 | tf_op jit(solution)/shard_map/gcm,gdn->mcdn/dot_general | solution.py:106
  561.9 0.7 copy-done
  563.3 0.8 fusion.27
  564.0 2.4 copy.52
  567.8 66.0 %all-reduce.3.cloned.1.call-done = f32[512,2,512]{2,1,0:T(2,128)} async-done(((f32[512,2,512]{2,1,0:T(2,128)}), f32[512,2,512]{2,1,0:T(2,128)}) %all-reduce.3.cloned.1.call-update) | async-done | bytes 2097168
  633.8 1.7 dynamic-slice_bitcast_fusion
  (32 shorter events, 5.6 us)
Async XLA Ops:
  26.8 134.1 %all-to-all-start = ((bf16[8,11,32,2,512]{4,3,2,1,0:T(2,128)(2,1)}), bf16[8,11,32,2,512]{4,3,2,1,0:T(2,128)(2,1)}, u32[]{:S(2)}, u32[]{:S(2)}) async-start(bf16[8,11,32,2,512]{4,3,2,1,0:T(2,128)(2,1)} %pack_left.3), calls=%async_computation | async-start | bytes 11534336 | tf_op jit(solution)/shard_map/all_to_all | solution.py:102
  160.9 132.4 %all-to-all-start.1 = ((bf16[8,11,32,2,512]{4,3,2,1,0:T(2,128)(2,1)}), bf16[8,11,32,2,512]{4,3,2,1,0:T(2,128)(2,1)}, u32[]{:S(2)}, u32[]{:S(2)}) async-start(bf16[8,11,32,2,512]{4,3,2,1,0:T(2,128)(2,1)} %pack_left.4), calls=%async_computation.1 | async-start | bytes 11534336 | tf_op jit(solution)/shard_map/all_to_all | solution.py:102
  177.5 127.5 %collective-permute-start = (bf16[8,11,32,2,512]{4,3,2,1,0:T(2,128)(2,1)}, bf16[8,11,32,2,512]{4,3,2,1,0:T(2,128)(2,1)}, u32[]{:S(2)}, u32[]{:S(2)}) collective-permute-start(bf16[8,11,32,2,512]{4,3,2,1,0:T(2,128)(2,1)} %pack_right.3), channel_id=1, source_target_pairs={{0,24},{8,0},{16,8},{24,16},{1,25},{9,1},{17,9},{25,17},{2,26},{10... | collective-permute-start | bytes 17301512 | tf_op jit(solution)/shard_map/ppermute | solution.py:104
  189.1 239.4 %collective-permute-start.1 = (bf16[8,11,32,2,512]{4,3,2,1,0:T(2,128)(2,1)}, bf16[8,11,32,2,512]{4,3,2,1,0:T(2,128)(2,1)}, u32[]{:S(2)}, u32[]{:S(2)}) collective-permute-start(bf16[8,11,32,2,512]{4,3,2,1,0:T(2,128)(2,1)} %pack_right.4), channel_id=1, source_target_pairs={{0,24},{8,0},{16,8},{24,16},{1,25},{9,1},{17,9},{25,17},{2,26},{10... | collective-permute-start | bytes 17301512 | tf_op jit(solution)/shard_map/ppermute | solution.py:104
  198.8 352.7 %collective-permute-start.2 = (bf16[8,11,32,2,512]{4,3,2,1,0:T(2,128)(2,1)}, bf16[8,11,32,2,512]{4,3,2,1,0:T(2,128)(2,1)}, u32[]{:S(2)}, u32[]{:S(2)}) collective-permute-start(bf16[8,11,32,2,512]{4,3,2,1,0:T(2,128)(2,1)} %pack_right.5), channel_id=1, source_target_pairs={{0,24},{8,0},{16,8},{24,16},{1,25},{9,1},{17,9},{25,17},{2,26},{10... | collective-permute-start | bytes 17301512 | tf_op jit(solution)/shard_map/ppermute | solution.py:104
  293.3 258.2 %all-to-all-start.2 = ((bf16[8,11,32,2,512]{4,3,2,1,0:T(2,128)(2,1)}), bf16[8,11,32,2,512]{4,3,2,1,0:T(2,128)(2,1)}, u32[]{:S(2)}, u32[]{:S(2)}) async-start(bf16[8,11,32,2,512]{4,3,2,1,0:T(2,128)(2,1)} %pack_left.5), calls=%async_computation.2 | async-start | bytes 11534336 | tf_op jit(solution)/shard_map/all_to_all | solution.py:102
  298.0 335.8 %all-reduce.3.cloned.1.call-start = ((), (), s32[]{:S(2)}) async-start(), calls=%async_computation.3 | async-start | bytes 4194304
  561.4 1.2 copy-start
  561.4 1.5 copy-start.1
  561.4 1.8 copy-start.2
  563.3 3.2 copy-start.3
Sparse Core Ops, SparseCore 0:
  566.6 67.0 all-reduce.2

commit v2 on v1

v2 whole, which is shorter than its diff:
```python
import functools

import jax
import jax.numpy as jnp
from jax import lax
from jax.experimental import pallas as pl
from jax.experimental.pallas import tpu as pltpu
from jax.sharding import PartitionSpec as P


BLK = 32


def offset_order(shards):
    far = sorted(range(1, shards), key=lambda d: (abs(d - shards // 2), d))
    return far[:1] + [0] + far[1:]


def chunks(shards):
    order = offset_order(shards)
    width = max(1, shards // 8)
    return [order[i : i + width] for i in range(0, shards, width)]


def pack_kernel(offset, group, capacity, shards, rotate, table, place, *refs):
    ins, out = refs[:group], refs[group]
    slots = shards * capacity
    row = lax.rem(place[0] + offset + shards, shards)
    entry = row * capacity + pl.program_id(0) * group
    if not rotate:
        for d in range(group):
            out[d] = ins[d][...]
        return
    shifts = [table[slots + entry + d] for d in range(group)]
    left_ends = [table[2 * slots + entry + d] for d in range(group)]
    right_ends = [table[3 * slots + entry + d] for d in range(group)]

    @pl.loop(0, BLK, unroll=2)
    def _(p):
        for d in range(group):
            lane = (p - shifts[d]) & (BLK - 1)
            values = ins[d][lane]
            live = (lane < left_ends[d]) & (p < right_ends[d])
            out[d, p] = jnp.where(live, values, jnp.zeros_like(values))


def pack(source, table, place, offset, capacity, shards, rotate):
    bands = source.shape[-1]
    group = max(n for n in range(1, 12) if capacity % n == 0)

    def picked(d):
        def index(step, table, place):
            row = lax.rem(place[0] + offset + shards, shards)
            return table[row * capacity + step * group + d], 0, 0

        return index

    moved = capacity * BLK * 2 * bands * 2
    return pl.pallas_call(
        functools.partial(pack_kernel, offset, group, capacity, shards, rotate),
        grid_spec=pltpu.PrefetchScalarGridSpec(
            num_scalar_prefetch=2,
            grid=(capacity // group,),
            in_specs=[pl.BlockSpec((BLK, 2, bands), picked(d)) for d in range(group)],
            out_specs=pl.BlockSpec((group, BLK, 2, bands), lambda step, table, place: (step, 0, 0, 0)),
        ),
        out_shape=jax.ShapeDtypeStruct((capacity, BLK, 2, bands), source.dtype),
        cost_estimate=pl.CostEstimate(flops=4 * moved, bytes_accessed=2 * moved, transcendentals=0),
        name="pack_left" if rotate else "pack_right",
    )(table, place, *([source] * group))


def scatter_sum(total, shards):
    core = lax.axis_index("ga") % 2
    chip = lax.axis_index("ga") // 2
    chips = shards // 2
    pairs = total.reshape(chips, 2, *total.shape[1:])
    swap = [(s, s ^ 1) for s in range(shards)]
    theirs = lax.dynamic_index_in_dim(pairs, 1 - core, 1, keepdims=False)
    ours = lax.dynamic_index_in_dim(pairs, core, 1, keepdims=False)
    ours = ours + lax.ppermute(theirs, "ga", swap)
    result = lax.dynamic_index_in_dim(ours, chip, 0, keepdims=False)
    for step in range(1, chips):
        part = lax.dynamic_index_in_dim(ours, (chip + step) % chips, 0, keepdims=False)
        result = result + lax.ppermute(part, "ga", [(s, (s + 2 * step) % shards) for s in range(shards)])
    return result


def local(coeffs, counts, block_map, wrap):
    held = coeffs[0]
    lines, g_rows, _, bands = held.shape
    shards = lax.axis_size("ga")
    per_shard = g_rows // BLK
    blocks = block_map.shape[-1]
    capacity = blocks // (shards * shards) + 1
    k_total = counts.shape[0]
    k = lax.axis_index("ka")
    g = lax.axis_index("ga")
    k_next = (k + 1) % k_total
    k_prev = (k + k_total - 1) % k_total
    ids = jnp.arange(per_shard, dtype=jnp.int32)
    slot_ids = jnp.arange(capacity, dtype=jnp.int32)
    shard_ids = jnp.arange(shards, dtype=jnp.int32)
    place = g.astype(jnp.int32).reshape(1)
    down = [(s, (s - 1) % k_total) for s in range(k_total)]
    rows_here = bands // shards
    outs = []
    for line in range(lines):
        mine = lax.dynamic_slice_in_dim(block_map[k, line], g * per_shard, per_shard, 0)
        shift = lax.dynamic_slice_in_dim(wrap[k, line], g * per_shard, per_shard, 0)
        target = mine // per_shard
        rank = jnp.sum(
            ((target[:, None] == target[None, :]) & (ids[:, None] > ids[None, :])).astype(jnp.int32), axis=1
        )
        left_end = counts[k, line] - (g * g_rows + ids * BLK)
        right_end = counts[k_next, line] - mine * BLK
        hit = (target[None, None, :] == shard_ids[:, None, None]) & (rank[None, None, :] == slot_ids[None, :, None])
        values = jnp.stack([ids, shift, left_end, right_end])
        left_table = jnp.sum(jnp.where(hit[None], values[:, None, None, :], 0), axis=3).reshape(-1)
        theirs = block_map[k_prev, line].reshape(shards, per_shard)
        for_me = theirs // per_shard == g
        rank_in = jnp.sum((for_me[:, None, :] & (ids[:, None] > ids[None, :])[None]).astype(jnp.int32), axis=2)
        hit_in = for_me[:, None, :] & (rank_in[:, None, :] == slot_ids[None, :, None])
        right_table = jnp.sum(jnp.where(hit_in, (theirs % per_shard)[:, None, :], 0), axis=2).reshape(-1)

        rows = held[line]
        total = None
        for together in chunks(shards):
            lefts, rights = [], []
            for d in together:
                left = pack(rows, left_table, place, d, capacity, shards, True)
                left_table, right_table, left = lax.optimization_barrier((left_table, right_table, left))
                if d:
                    left = lax.ppermute(left, "ga", [(s, (s + d) % shards) for s in range(shards)])
                right = pack(rows, right_table, place, -d, capacity, shards, False)
                left_table, right_table, right = lax.optimization_barrier((left_table, right_table, right))
                right = lax.ppermute(right, "ka", down)
                lefts.append(left)
                rights.append(right)
            left = lefts[0] if len(lefts) == 1 else jnp.concatenate(lefts)
            right = rights[0] if len(rights) == 1 else jnp.concatenate(rights)
            count = len(together) * capacity * BLK
            products = jnp.einsum(
                "gcm,gdn->mcdn",
                left.reshape(count, 2, bands),
                right.reshape(count, 2, bands),
                preferred_element_type=jnp.float32,
            )
            part = jnp.stack(
                [products[:, 0, 0] + products[:, 1, 1], products[:, 0, 1] - products[:, 1, 0]], axis=1
            )
            total = part if total is None else total + part
        outs.append(scatter_sum(total.reshape(shards, rows_here, 2, bands), shards))
    return jnp.stack(outs, axis=1)[None]


def solution(mesh):
    placed = (P("ka", None, "ga", None, None), P(), P(), P())

    return jax.shard_map(
        local,
        mesh=mesh,
        in_specs=placed,
        out_specs=P("ka", "ga", None, None, None),
        check_vma=False,
    )
```

time: 647 us -> 534 us (0.83)
  waiting for transfers between devices: 492 us -> 285 us
  starting transfers between devices: 20.4 us -> 68.5 us
  Pallas kernels: 65.4 us -> 94.6 us
  matrix products: 29.8 us -> 54.4 us
  between operations: 14.3 us -> 0.73 us
    all_to_all x3 -> x0, waiting for transfers between devices: 196 us -> none  [local(): left = lax.all_to_all(sent, 'ga', split_axis=0, concat_axis=0, tiled=True)]
    ppermute x0 -> x11, waiting for transfers between devices: none -> 187 us  [the longest x7 163 us: local(): lax.ppermute(left, 'ga', [(s, (s + d) % shards) for s in range(shards)])]
    ppermute x3 -> x8, waiting for transfers between devices: 230 us -> 98.1 us  [local(): right = lax.ppermute(right, 'ka', down)]
    unnamed x2 -> x0, waiting for transfers between devices: 66 us -> none
    ppermute x0 -> x11, starting transfers between devices: none -> 57.9 us  [the longest x7 29.1 us: local(): lax.ppermute(left, 'ga', [(s, (s + d) % shards) for s in range(shards)])]
    pallas_call x6 -> x16, Pallas kernels: 65.4 us -> 94.6 us  [pack(): pl.pallas_call(functools.partial(pack_kernel, offset, group, capacity, sh...]
    dot_general x3 -> x8, matrix products: 29.8 us -> 54.4 us  [local(): jnp.einsum('gcm,gdn->mcdn', left.reshape(count, 2, bands), right.reshape(...]
    all_to_all x3 -> x0, starting transfers between devices: 15.7 us -> none  [local(): left = lax.all_to_all(sent, 'ga', split_axis=0, concat_axis=0, tiled=True)]
  transfers between devices with their start and end apart: 7 -> 19, of which waited for: 6 -> 9; matrix products, arithmetic and copies ran while one was open for 4% -> 10% of each run, Pallas kernels for 8% -> 14%
where the time goes in v2:
time: 534 us; the launch traced here: 525 us
  waiting for transfers between devices  285 us (53%)
  Pallas kernels  94.6 us (18%)
  starting transfers between devices  68.5 us (13%)
  matrix products  54.4 us (10%)
  other arithmetic  14 us (3%)
  local copies, waits for them, and re-layouts  7.12 us (1%)
    ppermute x7, waiting for transfers between devices, local(): lax.ppermute(left, 'ga', [(s, (s + d) % shards) for s in range(shards)])  163 us
    ppermute x8, waiting for transfers between devices, local(): right = lax.ppermute(right, 'ka', down)  98.1 us
    pallas_call x16, Pallas kernels, pack(): pl.pallas_call(functools.partial(pack_kernel, offset, group, capacity, sh...  94.6 us
    dot_general x8, matrix products, local(): jnp.einsum('gcm,gdn->mcdn', left.reshape(count, 2, bands), right.reshape(...  54.4 us
    ppermute x7, starting transfers between devices, local(): lax.ppermute(left, 'ga', [(s, (s + d) % shards) for s in range(shards)])  29.1 us
    ppermute x3, starting transfers between devices, scatter_sum(): lax.ppermute(part, 'ga', [(s, (s + 2 * step) % shards) for s in range(sha...  28.7 us
    ppermute x3, waiting for transfers between devices, scatter_sum(): lax.ppermute(part, 'ga', [(s, (s + 2 * step) % shards) for s in range(sha...  21.4 us
  transfers between devices with their start and end apart: 19, of which 9 were waited for; matrix products, arithmetic and copies ran while one was open for 10% of the time, Pallas kernels for 14%

profile of v2, /device:TPU:0, one launch (start us, length us, event | category | flops | bytes accessed | tf_op | source)
XLA Modules:
  0.0 524.6 jit_solution(5099814136219734100)
XLA Ops:
  10.2 7.3 %pack_left.8 = bf16[33,32,2,512]{3,2,1,0:T(2,128)(2,1)} custom-call(s32[1056]{0:T(1024)} %reshape.563.table, s32[1]{0:T(128)} %bitcast.6.place, bf16[8192,2,512]{2,1,0:T(2,128)(2,1)} %bitcast.166, bf16[8192,2,512]{2,1,0:T(2,128)(2,1)} %bitcast.167, bf16[8192,2,512]{2,1,0:T(2,128)(2,1)} %bitcast.168, bf16[8192,2,512]{2,1,0:T(2,128)(2,1)} %bitcast.169, ...), custom_call_target="tpu_custom_call" | custom-call | flops 8650752 | bytes 4325376 | tf_op jit(solution)/shard_map/pack_left/pallas_call | solution.py:59
  17.5 4.6 pack_right.8
  22.1 7.3 %pack_left.9 = bf16[33,32,2,512]{3,2,1,0:T(2,128)(2,1)} custom-call(s32[1056]{0:T(1024)} %reshape.563.table, s32[1]{0:T(128)} %bitcast.6.place, bf16[8192,2,512]{2,1,0:T(2,128)(2,1)} %bitcast.188, bf16[8192,2,512]{2,1,0:T(2,128)(2,1)} %bitcast.189, bf16[8192,2,512]{2,1,0:T(2,128)(2,1)} %bitcast.190, bf16[8192,2,512]{2,1,0:T(2,128)(2,1)} %bitcast.191, ...), custom_call_target="tpu_custom_call" | custom-call | flops 8650752 | bytes 4325376 | tf_op jit(solution)/shard_map/pack_left/pallas_call | solution.py:59
  41.0 7.2 %pack_left.10 = bf16[33,32,2,512]{3,2,1,0:T(2,128)(2,1)} custom-call(s32[1056]{0:T(1024)} %reshape.563.table, s32[1]{0:T(128)} %bitcast.6.place, bf16[8192,2,512]{2,1,0:T(2,128)(2,1)} %bitcast.210, bf16[8192,2,512]{2,1,0:T(2,128)(2,1)} %bitcast.211, bf16[8192,2,512]{2,1,0:T(2,128)(2,1)} %bitcast.212, bf16[8192,2,512]{2,1,0:T(2,128)(2,1)} %bitcast.213, ...), custom_call_target="tpu_custom_call" | custom-call | flops 8650752 | bytes 4325376 | tf_op jit(solution)/shard_map/pack_left/pallas_call | solution.py:59
  54.3 7.2 %pack_left.11 = bf16[33,32,2,512]{3,2,1,0:T(2,128)(2,1)} custom-call(s32[1056]{0:T(1024)} %reshape.563.table, s32[1]{0:T(128)} %bitcast.6.place, bf16[8192,2,512]{2,1,0:T(2,128)(2,1)} %bitcast.232, bf16[8192,2,512]{2,1,0:T(2,128)(2,1)} %bitcast.233, bf16[8192,2,512]{2,1,0:T(2,128)(2,1)} %bitcast.234, bf16[8192,2,512]{2,1,0:T(2,128)(2,1)} %bitcast.235, ...), custom_call_target="tpu_custom_call" | custom-call | flops 8650752 | bytes 4325376 | tf_op jit(solution)/shard_map/pack_left/pallas_call | solution.py:59
  61.6 4.6 pack_right.11
  66.1 7.2 %pack_left.12 = bf16[33,32,2,512]{3,2,1,0:T(2,128)(2,1)} custom-call(s32[1056]{0:T(1024)} %reshape.563.table, s32[1]{0:T(128)} %bitcast.6.place, bf16[8192,2,512]{2,1,0:T(2,128)(2,1)} %bitcast.254, bf16[8192,2,512]{2,1,0:T(2,128)(2,1)} %bitcast.255, bf16[8192,2,512]{2,1,0:T(2,128)(2,1)} %bitcast.256, bf16[8192,2,512]{2,1,0:T(2,128)(2,1)} %bitcast.257, ...), custom_call_target="tpu_custom_call" | custom-call | flops 8650752 | bytes 4325376 | tf_op jit(solution)/shard_map/pack_left/pallas_call | solution.py:59
  73.4 4.5 pack_right.12
  77.9 7.3 %pack_left.13 = bf16[33,32,2,512]{3,2,1,0:T(2,128)(2,1)} custom-call(s32[1056]{0:T(1024)} %reshape.563.table, s32[1]{0:T(128)} %bitcast.6.place, bf16[8192,2,512]{2,1,0:T(2,128)(2,1)} %bitcast.276, bf16[8192,2,512]{2,1,0:T(2,128)(2,1)} %bitcast.277, bf16[8192,2,512]{2,1,0:T(2,128)(2,1)} %bitcast.278, bf16[8192,2,512]{2,1,0:T(2,128)(2,1)} %bitcast.279, ...), custom_call_target="tpu_custom_call" | custom-call | flops 8650752 | bytes 4325376 | tf_op jit(solution)/shard_map/pack_left/pallas_call | solution.py:59
  85.2 4.5 pack_right.13
  89.7 7.3 %pack_left.14 = bf16[33,32,2,512]{3,2,1,0:T(2,128)(2,1)} custom-call(s32[1056]{0:T(1024)} %reshape.563.table, s32[1]{0:T(128)} %bitcast.6.place, bf16[8192,2,512]{2,1,0:T(2,128)(2,1)} %bitcast.298, bf16[8192,2,512]{2,1,0:T(2,128)(2,1)} %bitcast.299, bf16[8192,2,512]{2,1,0:T(2,128)(2,1)} %bitcast.300, bf16[8192,2,512]{2,1,0:T(2,128)(2,1)} %bitcast.301, ...), custom_call_target="tpu_custom_call" | custom-call | flops 8650752 | bytes 4325376 | tf_op jit(solution)/shard_map/pack_left/pallas_call | solution.py:59
  97.0 4.5 pack_right.14
  101.6 7.2 %pack_left.15 = bf16[33,32,2,512]{3,2,1,0:T(2,128)(2,1)} custom-call(s32[1056]{0:T(1024)} %reshape.563.table, s32[1]{0:T(128)} %bitcast.6.place, bf16[8192,2,512]{2,1,0:T(2,128)(2,1)} %bitcast.326, bf16[8192,2,512]{2,1,0:T(2,128)(2,1)} %bitcast.321, bf16[8192,2,512]{2,1,0:T(2,128)(2,1)} %bitcast.322, bf16[8192,2,512]{2,1,0:T(2,128)(2,1)} %bitcast.323, ...), custom_call_target="tpu_custom_call" | custom-call | flops 8650752 | bytes 4325376 | tf_op jit(solution)/shard_map/pack_left/pallas_call | solution.py:59
  108.8 4.7 pack_right.15
  116.2 7.5 %fusion.37 = f32[512,2,2,512]{3,0,1,2:T(8,128)S(1)} fusion(bf16[33,32,2,512]{3,2,1,0:T(2,128)(2,1)} %pack_left.9, bf16[33,32,2,512,1]{3,2,1,0,4:T(2,128)(2,1)} %bitcast.18), kind=kOutput, calls=%fused_computation.33 | convolution fusion | flops 2214592512 | bytes 8519680 | tf_op jit(solution)/shard_map/gcm,gdn->mcdn/dot_general | solution.py:143
  123.6 80.9 %collective-permute-done.1 = bf16[33,32,2,512]{3,2,1,0:T(2,128)(2,1)} collective-permute-done((bf16[33,32,2,512]{3,2,1,0:T(2,128)(2,1)}, bf16[33,32,2,512]{3,2,1,0:T(2,128)(2,1)}, u32[]{:S(2)}, u32[]{:S(2)}) %collective-permute-start.1) | collective-permute-done | bytes 2162720 | tf_op jit(solution)/shard_map/ppermute | solution.py:134
  205.1 7.3 %fusion.32 = f32[512,2,2,512]{3,0,1,2:T(8,128)S(1)} fusion(bf16[33,32,2,512]{3,2,1,0:T(2,128)(2,1)} %collective-permute-done.1, bf16[33,32,2,512,1]{3,2,1,0,4:T(2,128)(2,1)} %bitcast.8), kind=kOutput, calls=%fused_computation.32 | convolution fusion | flops 2214592512 | bytes 8519680 | tf_op jit(solution)/shard_map/gcm,gdn->mcdn/dot_general | solution.py:143
  212.9 82.2 %collective-permute-done.4 = bf16[33,32,2,512]{3,2,1,0:T(2,128)(2,1)} collective-permute-done((bf16[33,32,2,512]{3,2,1,0:T(2,128)(2,1)}, bf16[33,32,2,512]{3,2,1,0:T(2,128)(2,1)}, u32[]{:S(2)}, u32[]{:S(2)}) %collective-permute-start.4) | collective-permute-done | bytes 2162720 | tf_op jit(solution)/shard_map/ppermute | solution.py:134
  295.7 11.8 %collective-permute-start.10 = (bf16[33,32,2,512]{3,2,1,0:T(2,128)(2,1)S(1)}, bf16[33,32,2,512]{3,2,1,0:T(2,128)(2,1)S(1)}, u32[]{:S(2)}, u32[]{:S(2)}) collective-permute-start(bf16[33,32,2,512]{3,2,1,0:T(2,128)(2,1)S(1)} %copy-done.5), channel_id=1, source_target_pairs={{0,6},{1,7},{2,0},{3,1},{4,2},{5,3},{6,4},{7,5},{8,14},{9,15},{10,... | collective-permute-start | bytes 6488072 | tf_op jit(solution)/shard_map/ppermute | solution.py:134
  307.5 7.3 %fusion.42 = f32[512,2,2,512]{3,0,1,2:T(8,128)S(1)} fusion(bf16[33,32,2,512]{3,2,1,0:T(2,128)(2,1)} %collective-permute-done.4, bf16[33,32,2,512,1]{3,2,1,0,4:T(2,128)(2,1)} %bitcast.28), kind=kOutput, calls=%fused_computation.34 | convolution fusion | flops 2214592512 | bytes 8519680 | tf_op jit(solution)/shard_map/gcm,gdn->mcdn/dot_general | solution.py:143
  319.7 6.8 %fusion.47 = f32[512,2,2,512]{3,0,1,2:T(8,128)S(1)} fusion(bf16[33,32,2,512]{3,2,1,0:T(2,128)(2,1)S(1)} %collective-permute-done.6, bf16[33,32,2,512,1]{3,2,1,0,4:T(2,128)(2,1)} %bitcast.360), kind=kOutput, calls=%fused_computation.35 | convolution fusion | flops 2214592512 | bytes 8519680 | tf_op jit(solution)/shard_map/gcm,gdn->mcdn/dot_general | solution.py:143
  327.6 16.6 %collective-permute-done.7 = bf16[33,32,2,512]{3,2,1,0:T(2,128)(2,1)} collective-permute-done((bf16[33,32,2,512]{3,2,1,0:T(2,128)(2,1)S(1)}, bf16[33,32,2,512]{3,2,1,0:T(2,128)(2,1)}, u32[]{:S(2)}, u32[]{:S(2)}) %collective-permute-start.7) | collective-permute-done | bytes 2162720 | tf_op jit(solution)/shard_map/ppermute | solution.py:137
  344.2 11.9 %collective-permute-start.14 = (bf16[33,32,2,512]{3,2,1,0:T(2,128)(2,1)S(1)}, bf16[33,32,2,512]{3,2,1,0:T(2,128)(2,1)S(1)}, u32[]{:S(2)}, u32[]{:S(2)}) collective-permute-start(bf16[33,32,2,512]{3,2,1,0:T(2,128)(2,1)S(1)} %copy-done.1), channel_id=1, source_target_pairs={{0,7},{1,0},{2,1},{3,2},{4,3},{5,4},{6,5},{7,6},{8,15},{9,8},{10,9... | collective-permute-start | bytes 6488072 | tf_op jit(solution)/shard_map/ppermute | solution.py:134
  356.1 6.8 %fusion.52 = f32[512,2,2,512]{3,0,1,2:T(8,128)S(1)} fusion(bf16[33,32,2,512]{3,2,1,0:T(2,128)(2,1)S(1)} %collective-permute-done.8, bf16[33,32,2,512,1]{3,2,1,0,4:T(2,128)(2,1)} %bitcast.48), kind=kOutput, calls=%fused_computation.36 | convolution fusion | flops 2214592512 | bytes 8519680 | tf_op jit(solution)/shard_map/gcm,gdn->mcdn/dot_general | solution.py:143
  365.1 17.6 %collective-permute-done.9 = bf16[33,32,2,512]{3,2,1,0:T(2,128)(2,1)} collective-permute-done((bf16[33,32,2,512]{3,2,1,0:T(2,128)(2,1)S(1)}, bf16[33,32,2,512]{3,2,1,0:T(2,128)(2,1)}, u32[]{:S(2)}, u32[]{:S(2)}) %collective-permute-start.9) | collective-permute-done | bytes 2162720 | tf_op jit(solution)/shard_map/ppermute | solution.py:137
  382.7 6.7 %fusion.57 = f32[512,2,2,512]{3,0,1,2:T(8,128)S(1)} fusion(bf16[33,32,2,512]{3,2,1,0:T(2,128)(2,1)S(1)} %collective-permute-done.10, bf16[33,32,2,512,1]{3,2,1,0,4:T(2,128)(2,1)} %bitcast.58), kind=kOutput, calls=%fused_computation.37 | convolution fusion | flops 2214592512 | bytes 8519680 | tf_op jit(solution)/shard_map/gcm,gdn->mcdn/dot_general | solution.py:143
  389.9 39.2 %collective-permute-done.11 = bf16[33,32,2,512]{3,2,1,0:T(2,128)(2,1)} collective-permute-done((bf16[33,32,2,512]{3,2,1,0:T(2,128)(2,1)S(1)}, bf16[33,32,2,512]{3,2,1,0:T(2,128)(2,1)}, u32[]{:S(2)}, u32[]{:S(2)}) %collective-permute-start.11) | collective-permute-done | bytes 2162720 | tf_op jit(solution)/shard_map/ppermute | solution.py:137
  429.0 6.7 %fusion.62 = f32[512,2,2,512]{3,0,1,2:T(8,128)S(1)} fusion(bf16[33,32,2,512]{3,2,1,0:T(2,128)(2,1)S(1)} %collective-permute-done.12, bf16[33,32,2,512,1]{3,2,1,0,4:T(2,128)(2,1)} %bitcast.68), kind=kOutput, calls=%fused_computation.38 | convolution fusion | flops 2214592512 | bytes 8519680 | tf_op jit(solution)/shard_map/gcm,gdn->mcdn/dot_general | solution.py:143
  436.2 24.7 %collective-permute-done.13 = bf16[33,32,2,512]{3,2,1,0:T(2,128)(2,1)S(1)} collective-permute-done((bf16[33,32,2,512]{3,2,1,0:T(2,128)(2,1)S(1)}, bf16[33,32,2,512]{3,2,1,0:T(2,128)(2,1)S(1)}, u32[]{:S(2)}, u32[]{:S(2)}) %collective-permute-start.13) | collective-permute-done | bytes 2162720 | tf_op jit(solution)/shard_map/ppermute | solution.py:137
  460.9 5.2 fusion.67
  476.0 24.0 %collective-permute-start.17 = (f32[64,2,512]{2,0,1:T(8,128)S(1)}, f32[64,2,512]{2,0,1:T(8,128)S(1)}, u32[]{:S(2)}, u32[]{:S(2)}) collective-permute-start(f32[64,2,512]{2,0,1:T(8,128)S(1)} %get-tuple-element.115), channel_id=1, source_target_pairs={{0,4},{1,5},{2,6},{3,7},{4,0},{5,1},{6,2},{7,3},{8,12},{9,13},{10,... | collective-permute-start | bytes 786440 | tf_op jit(solution)/shard_map/ppermute | solution.py:85
  504.6 18.8 %collective-permute-done.17 = f32[64,2,512]{2,0,1:T(8,128)S(1)} collective-permute-done((f32[64,2,512]{2,0,1:T(8,128)S(1)}, f32[64,2,512]{2,0,1:T(8,128)S(1)}, u32[]{:S(2)}, u32[]{:S(2)}) %collective-permute-start.17) | collective-permute-done | bytes 262176 | tf_op jit(solution)/shard_map/ppermute | solution.py:85
  (89 shorter events, 56.4 us)
Async XLA Ops:
  33.9 79.6 %collective-permute-start.2 = (bf16[33,32,2,512]{3,2,1,0:T(2,128)(2,1)}, bf16[33,32,2,512]{3,2,1,0:T(2,128)(2,1)}, u32[]{:S(2)}, u32[]{:S(2)}) collective-permute-start(bf16[33,32,2,512]{3,2,1,0:T(2,128)(2,1)} %pack_right.9), channel_id=1, source_target_pairs={{0,24},{8,0},{16,8},{24,16},{1,25},{9,1},{17,9},{25,17},{2,26},{10... | collective-permute-start | bytes 6488072 | tf_op jit(solution)/shard_map/ppermute | solution.py:137
  37.8 166.7 %collective-permute-start.1 = (bf16[33,32,2,512]{3,2,1,0:T(2,128)(2,1)}, bf16[33,32,2,512]{3,2,1,0:T(2,128)(2,1)}, u32[]{:S(2)}, u32[]{:S(2)}) collective-permute-start(bf16[33,32,2,512]{3,2,1,0:T(2,128)(2,1)} %pack_left.8), channel_id=1, source_target_pairs={{0,4},{1,5},{2,6},{3,7},{4,0},{5,1},{6,2},{7,3},{8,12},{9,13},{10,... | collective-permute-start | bytes 6488072 | tf_op jit(solution)/shard_map/ppermute | solution.py:134
  40.4 164.7 %collective-permute-start = (bf16[33,32,2,512]{3,2,1,0:T(2,128)(2,1)}, bf16[33,32,2,512]{3,2,1,0:T(2,128)(2,1)}, u32[]{:S(2)}, u32[]{:S(2)}) collective-permute-start(bf16[33,32,2,512]{3,2,1,0:T(2,128)(2,1)} %pack_right.8), channel_id=1, source_target_pairs={{0,24},{8,0},{16,8},{24,16},{1,25},{9,1},{17,9},{25,17},{2,26},{10... | collective-permute-start | bytes 6488072 | tf_op jit(solution)/shard_map/ppermute | solution.py:137
  48.2 246.9 %collective-permute-start.4 = (bf16[33,32,2,512]{3,2,1,0:T(2,128)(2,1)}, bf16[33,32,2,512]{3,2,1,0:T(2,128)(2,1)}, u32[]{:S(2)}, u32[]{:S(2)}) collective-permute-start(bf16[33,32,2,512]{3,2,1,0:T(2,128)(2,1)} %pack_left.10), channel_id=1, source_target_pairs={{0,3},{1,4},{2,5},{3,6},{4,7},{5,0},{6,1},{7,2},{8,11},{9,12},{10,... | collective-permute-start | bytes 6488072 | tf_op jit(solution)/shard_map/ppermute | solution.py:134
  52.9 242.8 %collective-permute-start.3 = (bf16[33,32,2,512]{3,2,1,0:T(2,128)(2,1)}, bf16[33,32,2,512]{3,2,1,0:T(2,128)(2,1)}, u32[]{:S(2)}, u32[]{:S(2)}) collective-permute-start(bf16[33,32,2,512]{3,2,1,0:T(2,128)(2,1)} %pack_right.10), channel_id=1, source_target_pairs={{0,24},{8,0},{16,8},{24,16},{1,25},{9,1},{17,9},{25,17},{2,26},{10... | collective-permute-start | bytes 6488072 | tf_op jit(solution)/shard_map/ppermute | solution.py:137
  108.8 4.7 copy-start.9
  113.5 201.8 %collective-permute-start.6 = (bf16[33,32,2,512]{3,2,1,0:T(2,128)(2,1)S(1)}, bf16[33,32,2,512]{3,2,1,0:T(2,128)(2,1)S(1)}, u32[]{:S(2)}, u32[]{:S(2)}) collective-permute-start(bf16[33,32,2,512]{3,2,1,0:T(2,128)(2,1)S(1)} %copy-done.9), channel_id=1, source_target_pairs={{0,5},{1,6},{2,7},{3,0},{4,1},{5,2},{6,3},{7,4},{8,13},{9,14},{10,... | collective-permute-start | bytes 6488072 | tf_op jit(solution)/shard_map/ppermute | solution.py:134
  116.2 88.4 %copy-start.8 = (bf16[33,32,2,512]{3,2,1,0:T(2,128)(2,1)S(1)}, bf16[33,32,2,512]{3,2,1,0:T(2,128)(2,1)}, u32[]{:S(2)}) copy-start(bf16[33,32,2,512]{3,2,1,0:T(2,128)(2,1)} %pack_right.11) | copy-start | bytes 6488068
  116.2 88.9 %copy-start.7 = (bf16[33,32,2,512]{3,2,1,0:T(2,128)(2,1)S(1)}, bf16[33,32,2,512]{3,2,1,0:T(2,128)(2,1)}, u32[]{:S(2)}) copy-start(bf16[33,32,2,512]{3,2,1,0:T(2,128)(2,1)} %pack_left.12) | copy-start | bytes 6488068
  204.6 113.8 %collective-permute-start.5 = (bf16[33,32,2,512]{3,2,1,0:T(2,128)(2,1)S(1)}, bf16[33,32,2,512]{3,2,1,0:T(2,128)(2,1)S(1)}, u32[]{:S(2)}, u32[]{:S(2)}) collective-permute-start(bf16[33,32,2,512]{3,2,1,0:T(2,128)(2,1)S(1)} %copy-done.8), channel_id=1, source_target_pairs={{0,24},{8,0},{16,8},{24,16},{1,25},{9,1},{17,9},{25,17},{2,26},{10... | collective-permute-start | bytes 6488072 | tf_op jit(solution)/shard_map/ppermute | solution.py:137
  205.1 121.4 %collective-permute-start.8 = (bf16[33,32,2,512]{3,2,1,0:T(2,128)(2,1)S(1)}, bf16[33,32,2,512]{3,2,1,0:T(2,128)(2,1)S(1)}, u32[]{:S(2)}, u32[]{:S(2)}) collective-permute-start(bf16[33,32,2,512]{3,2,1,0:T(2,128)(2,1)S(1)} %copy-done.7), channel_id=1, source_target_pairs={{0,2},{1,3},{2,4},{3,5},{4,6},{5,7},{6,0},{7,1},{8,10},{9,11},{10,... | collective-permute-start | bytes 6488072 | tf_op jit(solution)/shard_map/ppermute | solution.py:134
  212.4 82.7 %copy-start.6 = (bf16[33,32,2,512]{3,2,1,0:T(2,128)(2,1)S(1)}, bf16[33,32,2,512]{3,2,1,0:T(2,128)(2,1)}, u32[]{:S(2)}) copy-start(bf16[33,32,2,512]{3,2,1,0:T(2,128)(2,1)} %pack_right.12) | copy-start | bytes 6488068
  212.4 83.2 %copy-start.5 = (bf16[33,32,2,512]{3,2,1,0:T(2,128)(2,1)S(1)}, bf16[33,32,2,512]{3,2,1,0:T(2,128)(2,1)}, u32[]{:S(2)}) copy-start(bf16[33,32,2,512]{3,2,1,0:T(2,128)(2,1)} %pack_left.13) | copy-start | bytes 6488068
  295.1 49.1 %collective-permute-start.7 = (bf16[33,32,2,512]{3,2,1,0:T(2,128)(2,1)S(1)}, bf16[33,32,2,512]{3,2,1,0:T(2,128)(2,1)}, u32[]{:S(2)}, u32[]{:S(2)}) collective-permute-start(bf16[33,32,2,512]{3,2,1,0:T(2,128)(2,1)S(1)} %copy-done.6), channel_id=1, source_target_pairs={{0,24},{8,0},{16,8},{24,16},{1,25},{9,1},{17,9},{25,17},{2,26},{10... | collective-permute-start | bytes 6488072 | tf_op jit(solution)/shard_map/ppermute | solution.py:137
  295.7 67.3 %collective-permute-start.10 = (bf16[33,32,2,512]{3,2,1,0:T(2,128)(2,1)S(1)}, bf16[33,32,2,512]{3,2,1,0:T(2,128)(2,1)S(1)}, u32[]{:S(2)}, u32[]{:S(2)}) collective-permute-start(bf16[33,32,2,512]{3,2,1,0:T(2,128)(2,1)S(1)} %copy-done.5), channel_id=1, source_target_pairs={{0,6},{1,7},{2,0},{3,1},{4,2},{5,3},{6,4},{7,5},{8,14},{9,15},{10,... | collective-permute-start | bytes 6488072 | tf_op jit(solution)/shard_map/ppermute | solution.py:134
  314.8 1.6 copy-start.4
  315.3 3.0 copy-start.3
  316.4 66.3 %collective-permute-start.9 = (bf16[33,32,2,512]{3,2,1,0:T(2,128)(2,1)S(1)}, bf16[33,32,2,512]{3,2,1,0:T(2,128)(2,1)}, u32[]{:S(2)}, u32[]{:S(2)}) collective-permute-start(bf16[33,32,2,512]{3,2,1,0:T(2,128)(2,1)S(1)} %copy-done.4), channel_id=1, source_target_pairs={{0,24},{8,0},{16,8},{24,16},{1,25},{9,1},{17,9},{25,17},{2,26},{10... | collective-permute-start | bytes 6488072 | tf_op jit(solution)/shard_map/ppermute | solution.py:137
  318.3 1.3 copy-start.10
  318.4 71.5 %collective-permute-start.12 = (bf16[33,32,2,512]{3,2,1,0:T(2,128)(2,1)S(1)}, bf16[33,32,2,512]{3,2,1,0:T(2,128)(2,1)S(1)}, u32[]{:S(2)}, u32[]{:S(2)}) collective-permute-start(bf16[33,32,2,512]{3,2,1,0:T(2,128)(2,1)S(1)} %copy-done.3), channel_id=1, source_target_pairs={{0,1},{1,2},{2,3},{3,4},{4,5},{5,6},{6,7},{7,0},{8,9},{9,10},{10,1... | collective-permute-start | bytes 6488072 | tf_op jit(solution)/shard_map/ppermute | solution.py:134
  319.7 6.9 %copy-start.2 = (bf16[33,32,2,512]{3,2,1,0:T(2,128)(2,1)S(1)}, bf16[33,32,2,512]{3,2,1,0:T(2,128)(2,1)}, u32[]{:S(2)}) copy-start(bf16[33,32,2,512]{3,2,1,0:T(2,128)(2,1)} %pack_right.14) | copy-start | bytes 6488068
  326.5 17.7 %copy-start.1 = (bf16[33,32,2,512]{3,2,1,0:T(2,128)(2,1)S(1)}, bf16[33,32,2,512]{3,2,1,0:T(2,128)(2,1)}, u32[]{:S(2)}) copy-start(bf16[33,32,2,512]{3,2,1,0:T(2,128)(2,1)} %pack_left.15) | copy-start | bytes 6488068
  326.6 102.5 %collective-permute-start.11 = (bf16[33,32,2,512]{3,2,1,0:T(2,128)(2,1)S(1)}, bf16[33,32,2,512]{3,2,1,0:T(2,128)(2,1)}, u32[]{:S(2)}, u32[]{:S(2)}) collective-permute-start(bf16[33,32,2,512]{3,2,1,0:T(2,128)(2,1)S(1)} %copy-done.2), channel_id=1, source_target_pairs={{0,24},{8,0},{16,8},{24,16},{1,25},{9,1},{17,9},{25,17},{2,26},{10... | collective-permute-start | bytes 6488072 | tf_op jit(solution)/shard_map/ppermute | solution.py:137
  344.2 92.0 %collective-permute-start.14 = (bf16[33,32,2,512]{3,2,1,0:T(2,128)(2,1)S(1)}, bf16[33,32,2,512]{3,2,1,0:T(2,128)(2,1)S(1)}, u32[]{:S(2)}, u32[]{:S(2)}) collective-permute-start(bf16[33,32,2,512]{3,2,1,0:T(2,128)(2,1)S(1)} %copy-done.1), channel_id=1, source_target_pairs={{0,7},{1,0},{2,1},{3,2},{4,3},{5,4},{6,5},{7,6},{8,15},{9,8},{10,9... | collective-permute-start | bytes 6488072 | tf_op jit(solution)/shard_map/ppermute | solution.py:134
  356.1 6.9 %copy-start = (bf16[33,32,2,512]{3,2,1,0:T(2,128)(2,1)S(1)}, bf16[33,32,2,512]{3,2,1,0:T(2,128)(2,1)}, u32[]{:S(2)}) copy-start(bf16[33,32,2,512]{3,2,1,0:T(2,128)(2,1)} %pack_right.15) | copy-start | bytes 6488068
  363.0 98.0 %collective-permute-start.13 = (bf16[33,32,2,512]{3,2,1,0:T(2,128)(2,1)S(1)}, bf16[33,32,2,512]{3,2,1,0:T(2,128)(2,1)S(1)}, u32[]{:S(2)}, u32[]{:S(2)}) collective-permute-start(bf16[33,32,2,512]{3,2,1,0:T(2,128)(2,1)S(1)} %copy-done), channel_id=1, source_target_pairs={{0,24},{8,0},{16,8},{24,16},{1,25},{9,1},{17,9},{25,17},{2,26},{10... | collective-permute-start | bytes 6488072 | tf_op jit(solution)/shard_map/ppermute | solution.py:137
  468.9 2.9 collective-permute-start.15
  473.2 31.4 %collective-permute-start.18 = (f32[64,2,512]{2,0,1:T(8,128)S(1)}, f32[64,2,512]{2,0,1:T(8,128)S(1)}, u32[]{:S(2)}, u32[]{:S(2)}) collective-permute-start(f32[64,2,512]{2,0,1:T(8,128)S(1)} %get-tuple-element.114), channel_id=1, source_target_pairs={{0,6},{1,7},{2,0},{3,1},{4,2},{5,3},{6,4},{7,5},{8,14},{9,15},{10,... | collective-permute-start | bytes 786440 | tf_op jit(solution)/shard_map/ppermute | solution.py:85
  476.0 47.3 %collective-permute-start.17 = (f32[64,2,512]{2,0,1:T(8,128)S(1)}, f32[64,2,512]{2,0,1:T(8,128)S(1)}, u32[]{:S(2)}, u32[]{:S(2)}) collective-permute-start(f32[64,2,512]{2,0,1:T(8,128)S(1)} %get-tuple-element.115), channel_id=1, source_target_pairs={{0,4},{1,5},{2,6},{3,7},{4,0},{5,1},{6,2},{7,3},{8,12},{9,13},{10,... | collective-permute-start | bytes 786440 | tf_op jit(solution)/shard_map/ppermute | solution.py:85
  500.0 23.4 %collective-permute-start.16 = (f32[64,2,512]{2,0,1:T(8,128)S(1)}, f32[64,2,512]{2,0,1:T(8,128)S(1)}, u32[]{:S(2)}, u32[]{:S(2)}) collective-permute-start(f32[64,2,512]{2,0,1:T(8,128)S(1)} %get-tuple-element.113), channel_id=1, source_target_pairs={{0,2},{1,3},{2,4},{3,5},{4,6},{5,7},{6,0},{7,1},{8,10},{9,11},{10,... | collective-permute-start | bytes 786440 | tf_op jit(solution)/shard_map/ppermute | solution.py:85

commit v3 on v2

--- a/solution.py
+++ b/solution.py
@@ -71,18 +71,23 @@
 
 
 def scatter_sum(total, shards):
-    core = lax.axis_index("ga") % 2
-    chip = lax.axis_index("ga") // 2
-    chips = shards // 2
-    pairs = total.reshape(chips, 2, *total.shape[1:])
-    swap = [(s, s ^ 1) for s in range(shards)]
-    theirs = lax.dynamic_index_in_dim(pairs, 1 - core, 1, keepdims=False)
-    ours = lax.dynamic_index_in_dim(pairs, core, 1, keepdims=False)
-    ours = ours + lax.ppermute(theirs, "ga", swap)
-    result = lax.dynamic_index_in_dim(ours, chip, 0, keepdims=False)
-    for step in range(1, chips):
-        part = lax.dynamic_index_in_dim(ours, (chip + step) % chips, 0, keepdims=False)
-        result = result + lax.ppermute(part, "ga", [(s, (s + 2 * step) % shards) for s in range(shards)])
+    place = lax.axis_index("ga")
+    span = 1
+    while shards % (2 * span) == 0 and span < shards:
+        bit = (place // span) % 2
+        pairs = total.reshape(-1, 2, *total.shape[1:])
+        theirs = lax.dynamic_index_in_dim(pairs, 1 - bit, 1, keepdims=False)
+        ours = lax.dynamic_index_in_dim(pairs, bit, 1, keepdims=False)
+        total = ours + lax.ppermute(theirs, "ga", [(s, s ^ span) for s in range(shards)])
+        span *= 2
+    if span == shards:
+        return total[0]
+    place = place // span
+    rest = shards // span
+    result = lax.dynamic_index_in_dim(total, place, 0, keepdims=False)
+    for step in range(1, rest):
+        part = lax.dynamic_index_in_dim(total, (place + step) % rest, 0, keepdims=False)
+        result = result + lax.ppermute(part, "ga", [(s, (s + span * step) % shards) for s in range(shards)])
     return result
 
 
@@ -128,13 +133,13 @@
         for together in chunks(shards):
             lefts, rights = [], []
             for d in together:
+                right = pack(rows, right_table, place, -d, capacity, shards, False)
+                left_table, right_table, right = lax.optimization_barrier((left_table, right_table, right))
+                right = lax.ppermute(right, "ka", down)
                 left = pack(rows, left_table, place, d, capacity, shards, True)
                 left_table, right_table, left = lax.optimization_barrier((left_table, right_table, left))
                 if d:
                     left = lax.ppermute(left, "ga", [(s, (s + d) % shards) for s in range(shards)])
-                right = pack(rows, right_table, place, -d, capacity, shards, False)
-                left_table, right_table, right = lax.optimization_barrier((left_table, right_table, right))
-                right = lax.ppermute(right, "ka", down)
                 lefts.append(left)
                 rights.append(right)
             left = lefts[0] if len(lefts) == 1 else jnp.concatenate(lefts)

time: 534 us -> 531 us (level)
    ppermute x7, waiting for transfers between devices: 163 us -> 156 us  [local(): lax.ppermute(left, 'ga', [(s, (s + d) % shards) for s in range(shards)])]
    ppermute x4 -> x3, waiting for transfers between devices: 24.1 us -> 26.2 us  [scatter_sum(): lax.ppermute(theirs, 'ga', [(s, s ^ span) for s in range(shards)])]
    ppermute x4 -> x3, starting transfers between devices: 28.8 us -> 28.6 us  [scatter_sum(): lax.ppermute(theirs, 'ga', [(s, s ^ span) for s in range(shards)])]
  transfers between devices with their start and end apart: 19 -> 18, of which waited for: 9 -> 9; matrix products, arithmetic and copies ran while one was open for 10% -> 10% of each run, Pallas kernels for 14% -> 15%
where the time goes in v3:
time: 531 us; the launch traced here: 522 us
  waiting for transfers between devices  280 us (53%)
  Pallas kernels  94.6 us (18%)
  starting transfers between devices  68.3 us (13%)
  matrix products  56.6 us (11%)
  other arithmetic  12.7 us (2%)
  local copies, waits for them, and re-layouts  8.78 us (2%)
    ppermute x7, waiting for transfers between devices, local(): lax.ppermute(left, 'ga', [(s, (s + d) % shards) for s in range(shards)])  156 us
    ppermute x8, waiting for transfers between devices, local(): right = lax.ppermute(right, 'ka', down)  97.9 us
    pallas_call x16, Pallas kernels, pack(): pl.pallas_call(functools.partial(pack_kernel, offset, group, capacity, sh...  94.6 us
    dot_general x8, matrix products, local(): jnp.einsum('gcm,gdn->mcdn', left.reshape(count, 2, bands), right.reshape(...  56.6 us
    ppermute x7, starting transfers between devices, local(): lax.ppermute(left, 'ga', [(s, (s + d) % shards) for s in range(shards)])  29.2 us
    ppermute x3, starting transfers between devices, scatter_sum(): lax.ppermute(theirs, 'ga', [(s, s ^ span) for s in range(shards)])  28.6 us
    ppermute x3, waiting for transfers between devices, scatter_sum(): lax.ppermute(theirs, 'ga', [(s, s ^ span) for s in range(shards)])  26.2 us
  transfers between devices with their start and end apart: 18, of which 9 were waited for; matrix products, arithmetic and copies ran while one was open for 10% of the time, Pallas kernels for 15%

profile of v3, /device:TPU:0, one launch (start us, length us, event | category | flops | bytes accessed | tf_op | source)
XLA Modules:
  0.0 521.7 jit_solution(4543003508960794256)
XLA Ops:
  14.8 7.2 %pack_left.8 = bf16[33,32,2,512]{3,2,1,0:T(2,128)(2,1)} custom-call(s32[1056]{0:T(1024)} %reshape.571.table, s32[1]{0:T(128)} %bitcast.6.place, bf16[8192,2,512]{2,1,0:T(2,128)(2,1)} %bitcast.142, bf16[8192,2,512]{2,1,0:T(2,128)(2,1)} %bitcast.138, bf16[8192,2,512]{2,1,0:T(2,128)(2,1)} %bitcast.139, bf16[8192,2,512]{2,1,0:T(2,128)(2,1)} %bitcast.140, ...), custom_call_target="tpu_custom_call" | custom-call | flops 8650752 | bytes 4325376 | tf_op jit(solution)/shard_map/pack_left/pallas_call | solution.py:59
  22.0 4.5 pack_right.9
  33.6 7.2 %pack_left.9 = bf16[33,32,2,512]{3,2,1,0:T(2,128)(2,1)} custom-call(s32[1056]{0:T(1024)} %reshape.571.table, s32[1]{0:T(128)} %bitcast.6.place, bf16[8192,2,512]{2,1,0:T(2,128)(2,1)} %bitcast.164, bf16[8192,2,512]{2,1,0:T(2,128)(2,1)} %bitcast.160, bf16[8192,2,512]{2,1,0:T(2,128)(2,1)} %bitcast.161, bf16[8192,2,512]{2,1,0:T(2,128)(2,1)} %bitcast.162, ...), custom_call_target="tpu_custom_call" | custom-call | flops 8650752 | bytes 4325376 | tf_op jit(solution)/shard_map/pack_left/pallas_call | solution.py:59
  40.9 4.6 pack_right.10
  45.4 7.2 %pack_left.10 = bf16[33,32,2,512]{3,2,1,0:T(2,128)(2,1)} custom-call(s32[1056]{0:T(1024)} %reshape.571.table, s32[1]{0:T(128)} %bitcast.6.place, bf16[8192,2,512]{2,1,0:T(2,128)(2,1)} %bitcast.181, bf16[8192,2,512]{2,1,0:T(2,128)(2,1)} %bitcast.182, bf16[8192,2,512]{2,1,0:T(2,128)(2,1)} %bitcast.183, bf16[8192,2,512]{2,1,0:T(2,128)(2,1)} %bitcast.184, ...), custom_call_target="tpu_custom_call" | custom-call | flops 8650752 | bytes 4325376 | tf_op jit(solution)/shard_map/pack_left/pallas_call | solution.py:59
  58.8 7.2 %pack_left.11 = bf16[33,32,2,512]{3,2,1,0:T(2,128)(2,1)} custom-call(s32[1056]{0:T(1024)} %reshape.571.table, s32[1]{0:T(128)} %bitcast.6.place, bf16[8192,2,512]{2,1,0:T(2,128)(2,1)} %bitcast.213, bf16[8192,2,512]{2,1,0:T(2,128)(2,1)} %bitcast.204, bf16[8192,2,512]{2,1,0:T(2,128)(2,1)} %bitcast.205, bf16[8192,2,512]{2,1,0:T(2,128)(2,1)} %bitcast.206, ...), custom_call_target="tpu_custom_call" | custom-call | flops 8650752 | bytes 4325376 | tf_op jit(solution)/shard_map/pack_left/pallas_call | solution.py:59
  66.1 4.6 pack_right.12
  70.6 7.3 %pack_left.12 = bf16[33,32,2,512]{3,2,1,0:T(2,128)(2,1)} custom-call(s32[1056]{0:T(1024)} %reshape.571.table, s32[1]{0:T(128)} %bitcast.6.place, bf16[8192,2,512]{2,1,0:T(2,128)(2,1)} %bitcast.225, bf16[8192,2,512]{2,1,0:T(2,128)(2,1)} %bitcast.226, bf16[8192,2,512]{2,1,0:T(2,128)(2,1)} %bitcast.227, bf16[8192,2,512]{2,1,0:T(2,128)(2,1)} %bitcast.228, ...), custom_call_target="tpu_custom_call" | custom-call | flops 8650752 | bytes 4325376 | tf_op jit(solution)/shard_map/pack_left/pallas_call | solution.py:59
  77.9 4.6 pack_right.13
  82.5 7.2 %pack_left.13 = bf16[33,32,2,512]{3,2,1,0:T(2,128)(2,1)} custom-call(s32[1056]{0:T(1024)} %reshape.571.table, s32[1]{0:T(128)} %bitcast.6.place, bf16[8192,2,512]{2,1,0:T(2,128)(2,1)} %bitcast.253, bf16[8192,2,512]{2,1,0:T(2,128)(2,1)} %bitcast.248, bf16[8192,2,512]{2,1,0:T(2,128)(2,1)} %bitcast.249, bf16[8192,2,512]{2,1,0:T(2,128)(2,1)} %bitcast.250, ...), custom_call_target="tpu_custom_call" | custom-call | flops 8650752 | bytes 4325376 | tf_op jit(solution)/shard_map/pack_left/pallas_call | solution.py:59
  89.8 4.6 pack_right.14
  94.3 7.2 %pack_left.14 = bf16[33,32,2,512]{3,2,1,0:T(2,128)(2,1)} custom-call(s32[1056]{0:T(1024)} %reshape.571.table, s32[1]{0:T(128)} %bitcast.6.place, bf16[8192,2,512]{2,1,0:T(2,128)(2,1)} %bitcast.275, bf16[8192,2,512]{2,1,0:T(2,128)(2,1)} %bitcast.270, bf16[8192,2,512]{2,1,0:T(2,128)(2,1)} %bitcast.271, bf16[8192,2,512]{2,1,0:T(2,128)(2,1)} %bitcast.272, ...), custom_call_target="tpu_custom_call" | custom-call | flops 8650752 | bytes 4325376 | tf_op jit(solution)/shard_map/pack_left/pallas_call | solution.py:59
  106.1 7.4 %pack_left.15 = bf16[33,32,2,512]{3,2,1,0:T(2,128)(2,1)} custom-call(s32[1056]{0:T(1024)} %reshape.571.table, s32[1]{0:T(128)} %bitcast.6.place, bf16[8192,2,512]{2,1,0:T(2,128)(2,1)} %bitcast.291, bf16[8192,2,512]{2,1,0:T(2,128)(2,1)} %bitcast.292, bf16[8192,2,512]{2,1,0:T(2,128)(2,1)} %bitcast.293, bf16[8192,2,512]{2,1,0:T(2,128)(2,1)} %bitcast.294, ...), custom_call_target="tpu_custom_call" | custom-call | flops 8650752 | bytes 4325376 | tf_op jit(solution)/shard_map/pack_left/pallas_call | solution.py:59
  116.2 7.5 %fusion.37 = f32[512,2,2,512]{3,0,1,2:T(8,128)S(1)} fusion(bf16[33,32,2,512]{3,2,1,0:T(2,128)(2,1)} %pack_left.9, bf16[33,32,2,512,1]{3,2,1,0,4:T(2,128)(2,1)} %bitcast.16), kind=kOutput, calls=%fused_computation.33 | convolution fusion | flops 2214592512 | bytes 8519680 | tf_op jit(solution)/shard_map/gcm,gdn->mcdn/dot_general | solution.py:148
  123.6 73.6 %collective-permute-done.1 = bf16[33,32,2,512]{3,2,1,0:T(2,128)(2,1)} collective-permute-done((bf16[33,32,2,512]{3,2,1,0:T(2,128)(2,1)}, bf16[33,32,2,512]{3,2,1,0:T(2,128)(2,1)}, u32[]{:S(2)}, u32[]{:S(2)}) %collective-permute-start.1) | collective-permute-done | bytes 2162720 | tf_op jit(solution)/shard_map/ppermute | solution.py:142
  197.8 7.3 %fusion.32 = f32[512,2,2,512]{3,0,1,2:T(8,128)S(1)} fusion(bf16[33,32,2,512]{3,2,1,0:T(2,128)(2,1)} %collective-permute-done.1, bf16[33,32,2,512,1]{3,2,1,0,4:T(2,128)(2,1)} %bitcast.8), kind=kOutput, calls=%fused_computation.32 | convolution fusion | flops 2214592512 | bytes 8519680 | tf_op jit(solution)/shard_map/gcm,gdn->mcdn/dot_general | solution.py:148
  205.6 82.2 %collective-permute-done.4 = bf16[33,32,2,512]{3,2,1,0:T(2,128)(2,1)} collective-permute-done((bf16[33,32,2,512]{3,2,1,0:T(2,128)(2,1)}, bf16[33,32,2,512]{3,2,1,0:T(2,128)(2,1)}, u32[]{:S(2)}, u32[]{:S(2)}) %collective-permute-start.4) | collective-permute-done | bytes 2162720 | tf_op jit(solution)/shard_map/ppermute | solution.py:142
  288.3 11.8 %collective-permute-start.10 = (bf16[33,32,2,512]{3,2,1,0:T(2,128)(2,1)S(1)}, bf16[33,32,2,512]{3,2,1,0:T(2,128)(2,1)S(1)}, u32[]{:S(2)}, u32[]{:S(2)}) collective-permute-start(bf16[33,32,2,512]{3,2,1,0:T(2,128)(2,1)S(1)} %copy-done.5), channel_id=1, source_target_pairs={{0,6},{1,7},{2,0},{3,1},{4,2},{5,3},{6,4},{7,5},{8,14},{9,15},{10,... | collective-permute-start | bytes 6488072 | tf_op jit(solution)/shard_map/ppermute | solution.py:142
  300.1 7.3 %fusion.42 = f32[512,2,2,512]{3,0,1,2:T(8,128)S(1)} fusion(bf16[33,32,2,512]{3,2,1,0:T(2,128)(2,1)} %collective-permute-done.4, bf16[33,32,2,512,1]{3,2,1,0,4:T(2,128)(2,1)} %bitcast.24), kind=kOutput, calls=%fused_computation.34 | convolution fusion | flops 2214592512 | bytes 8519680 | tf_op jit(solution)/shard_map/gcm,gdn->mcdn/dot_general | solution.py:148
  312.4 6.8 %fusion.47 = f32[512,2,2,512]{3,0,1,2:T(8,128)S(1)} fusion(bf16[33,32,2,512]{3,2,1,0:T(2,128)(2,1)S(1)} %collective-permute-done.6, bf16[33,32,2,512,1]{3,2,1,0,4:T(2,128)(2,1)} %bitcast.323), kind=kOutput, calls=%fused_computation.35 | convolution fusion | flops 2214592512 | bytes 8519680 | tf_op jit(solution)/shard_map/gcm,gdn->mcdn/dot_general | solution.py:148
  320.3 16.6 %collective-permute-done.7 = bf16[33,32,2,512]{3,2,1,0:T(2,128)(2,1)} collective-permute-done((bf16[33,32,2,512]{3,2,1,0:T(2,128)(2,1)S(1)}, bf16[33,32,2,512]{3,2,1,0:T(2,128)(2,1)}, u32[]{:S(2)}, u32[]{:S(2)}) %collective-permute-start.7) | collective-permute-done | bytes 2162720 | tf_op jit(solution)/shard_map/ppermute | solution.py:138
  336.9 11.9 %collective-permute-start.14 = (bf16[33,32,2,512]{3,2,1,0:T(2,128)(2,1)S(1)}, bf16[33,32,2,512]{3,2,1,0:T(2,128)(2,1)}, u32[]{:S(2)}, u32[]{:S(2)}) collective-permute-start(bf16[33,32,2,512]{3,2,1,0:T(2,128)(2,1)S(1)} %copy-done.1), channel_id=1, source_target_pairs={{0,7},{1,0},{2,1},{3,2},{4,3},{5,4},{6,5},{7,6},{8,15},{9,8},{10,9... | collective-permute-start | bytes 6488072 | tf_op jit(solution)/shard_map/ppermute | solution.py:142
  348.8 6.8 %fusion.52 = f32[512,2,2,512]{3,0,1,2:T(8,128)S(1)} fusion(bf16[33,32,2,512]{3,2,1,0:T(2,128)(2,1)S(1)} %collective-permute-done.8, bf16[33,32,2,512,1]{3,2,1,0,4:T(2,128)(2,1)} %bitcast.40), kind=kOutput, calls=%fused_computation.36 | convolution fusion | flops 2214592512 | bytes 8519680 | tf_op jit(solution)/shard_map/gcm,gdn->mcdn/dot_general | solution.py:148
  357.9 17.5 %collective-permute-done.9 = bf16[33,32,2,512]{3,2,1,0:T(2,128)(2,1)} collective-permute-done((bf16[33,32,2,512]{3,2,1,0:T(2,128)(2,1)S(1)}, bf16[33,32,2,512]{3,2,1,0:T(2,128)(2,1)}, u32[]{:S(2)}, u32[]{:S(2)}) %collective-permute-start.9) | collective-permute-done | bytes 2162720 | tf_op jit(solution)/shard_map/ppermute | solution.py:138
  375.4 6.7 %fusion.57 = f32[512,2,2,512]{3,0,1,2:T(8,128)S(1)} fusion(bf16[33,32,2,512]{3,2,1,0:T(2,128)(2,1)S(1)} %collective-permute-done.10, bf16[33,32,2,512,1]{3,2,1,0,4:T(2,128)(2,1)} %bitcast.48), kind=kOutput, calls=%fused_computation.37 | convolution fusion | flops 2214592512 | bytes 8519680 | tf_op jit(solution)/shard_map/gcm,gdn->mcdn/dot_general | solution.py:148
  382.5 39.2 %collective-permute-done.11 = bf16[33,32,2,512]{3,2,1,0:T(2,128)(2,1)} collective-permute-done((bf16[33,32,2,512]{3,2,1,0:T(2,128)(2,1)S(1)}, bf16[33,32,2,512]{3,2,1,0:T(2,128)(2,1)}, u32[]{:S(2)}, u32[]{:S(2)}) %collective-permute-start.11) | collective-permute-done | bytes 2162720 | tf_op jit(solution)/shard_map/ppermute | solution.py:138
  421.7 6.7 %fusion.62 = f32[512,2,2,512]{3,0,1,2:T(8,128)S(1)} fusion(bf16[33,32,2,512]{3,2,1,0:T(2,128)(2,1)S(1)} %collective-permute-done.12, bf16[33,32,2,512,1]{3,2,1,0,4:T(2,128)(2,1)} %bitcast.56), kind=kOutput, calls=%fused_computation.38 | convolution fusion | flops 2214592512 | bytes 8519680 | tf_op jit(solution)/shard_map/gcm,gdn->mcdn/dot_general | solution.py:148
  428.9 24.7 %collective-permute-done.13 = bf16[33,32,2,512]{3,2,1,0:T(2,128)(2,1)S(1)} collective-permute-done((bf16[33,32,2,512]{3,2,1,0:T(2,128)(2,1)S(1)}, bf16[33,32,2,512]{3,2,1,0:T(2,128)(2,1)S(1)}, u32[]{:S(2)}, u32[]{:S(2)}) %collective-permute-start.13) | collective-permute-done | bytes 2162720 | tf_op jit(solution)/shard_map/ppermute | solution.py:138
  454.9 7.5 %fusion.67 = f32[512,2,2,512]{3,0,1,2:T(8,128)S(1)} fusion(bf16[33,32,2,512]{3,2,1,0:T(2,128)(2,1)} %collective-permute-done.14, bf16[33,32,2,512,1]{3,2,1,0,4:T(2,128)(2,1)} %bitcast.324), kind=kOutput, calls=%fused_computation.39 | convolution fusion | flops 2214592512 | bytes 8519680 | tf_op jit(solution)/shard_map/gcm,gdn->mcdn/dot_general | solution.py:148
  468.4 24.8 %collective-permute-start.16 = (f32[2,64,2,512]{3,1,2,0:T(8,128)S(1)}, f32[2,64,2,512]{3,1,2,0:T(8,128)S(1)}, u32[]{:S(2)}, u32[]{:S(2)}) collective-permute-start(f32[2,64,2,512]{3,1,2,0:T(8,128)S(1)} %dynamic-slice_bitcast_fusion), channel_id=1, source_target_pairs={{0,2},{1,3},{2,0},{3,1},{4,6},{5,7},{6,4},{7,5},{8,10},{9,11},{10,... | collective-permute-start | bytes 1572872 | tf_op jit(solution)/shard_map/ppermute | solution.py:81
  493.1 12.2 %collective-permute-done.16 = f32[2,64,2,512]{3,1,2,0:T(8,128)S(1)} collective-permute-done((f32[2,64,2,512]{3,1,2,0:T(8,128)S(1)}, f32[2,64,2,512]{3,1,2,0:T(8,128)S(1)}, u32[]{:S(2)}, u32[]{:S(2)}) %collective-permute-start.16) | collective-permute-done | bytes 524320 | tf_op jit(solution)/shard_map/ppermute | solution.py:81
  509.2 11.4 %collective-permute-done.17 = f32[1,64,2,512]{3,1,2,0:T(8,128)S(1)} collective-permute-done((f32[1,64,2,512]{3,1,2,0:T(8,128)S(1)}, f32[1,64,2,512]{3,1,2,0:T(8,128)S(1)}, u32[]{:S(2)}, u32[]{:S(2)}) %collective-permute-start.17) | collective-permute-done | bytes 262176 | tf_op jit(solution)/shard_map/ppermute | solution.py:81
  (92 shorter events, 57.6 us)
Async XLA Ops:
  26.6 87.0 %collective-permute-start.2 = (bf16[33,32,2,512]{3,2,1,0:T(2,128)(2,1)}, bf16[33,32,2,512]{3,2,1,0:T(2,128)(2,1)}, u32[]{:S(2)}, u32[]{:S(2)}) collective-permute-start(bf16[33,32,2,512]{3,2,1,0:T(2,128)(2,1)} %pack_right.9), channel_id=1, source_target_pairs={{0,24},{8,0},{16,8},{24,16},{1,25},{9,1},{17,9},{25,17},{2,26},{10... | collective-permute-start | bytes 6488072 | tf_op jit(solution)/shard_map/ppermute | solution.py:138
  30.5 166.7 %collective-permute-start.1 = (bf16[33,32,2,512]{3,2,1,0:T(2,128)(2,1)}, bf16[33,32,2,512]{3,2,1,0:T(2,128)(2,1)}, u32[]{:S(2)}, u32[]{:S(2)}) collective-permute-start(bf16[33,32,2,512]{3,2,1,0:T(2,128)(2,1)} %pack_left.8), channel_id=1, source_target_pairs={{0,4},{1,5},{2,6},{3,7},{4,0},{5,1},{6,2},{7,3},{8,12},{9,13},{10,... | collective-permute-start | bytes 6488072 | tf_op jit(solution)/shard_map/ppermute | solution.py:142
  33.1 164.7 %collective-permute-start = (bf16[33,32,2,512]{3,2,1,0:T(2,128)(2,1)}, bf16[33,32,2,512]{3,2,1,0:T(2,128)(2,1)}, u32[]{:S(2)}, u32[]{:S(2)}) collective-permute-start(bf16[33,32,2,512]{3,2,1,0:T(2,128)(2,1)} %pack_right.8), channel_id=1, source_target_pairs={{0,24},{8,0},{16,8},{24,16},{1,25},{9,1},{17,9},{25,17},{2,26},{10... | collective-permute-start | bytes 6488072 | tf_op jit(solution)/shard_map/ppermute | solution.py:138
  52.7 235.1 %collective-permute-start.4 = (bf16[33,32,2,512]{3,2,1,0:T(2,128)(2,1)}, bf16[33,32,2,512]{3,2,1,0:T(2,128)(2,1)}, u32[]{:S(2)}, u32[]{:S(2)}) collective-permute-start(bf16[33,32,2,512]{3,2,1,0:T(2,128)(2,1)} %pack_left.10), channel_id=1, source_target_pairs={{0,3},{1,4},{2,5},{3,6},{4,7},{5,0},{6,1},{7,2},{8,11},{9,12},{10,... | collective-permute-start | bytes 6488072 | tf_op jit(solution)/shard_map/ppermute | solution.py:142
  52.9 235.5 %collective-permute-start.3 = (bf16[33,32,2,512]{3,2,1,0:T(2,128)(2,1)}, bf16[33,32,2,512]{3,2,1,0:T(2,128)(2,1)}, u32[]{:S(2)}, u32[]{:S(2)}) collective-permute-start(bf16[33,32,2,512]{3,2,1,0:T(2,128)(2,1)} %pack_right.10), channel_id=1, source_target_pairs={{0,24},{8,0},{16,8},{24,16},{1,25},{9,1},{17,9},{25,17},{2,26},{10... | collective-permute-start | bytes 6488072 | tf_op jit(solution)/shard_map/ppermute | solution.py:138
  106.1 7.4 %copy-start.9 = (bf16[33,32,2,512]{3,2,1,0:T(2,128)(2,1)S(1)}, bf16[33,32,2,512]{3,2,1,0:T(2,128)(2,1)}, u32[]{:S(2)}) copy-start(bf16[33,32,2,512]{3,2,1,0:T(2,128)(2,1)} %pack_left.11) | copy-start | bytes 6488068
  113.5 194.4 %collective-permute-start.6 = (bf16[33,32,2,512]{3,2,1,0:T(2,128)(2,1)S(1)}, bf16[33,32,2,512]{3,2,1,0:T(2,128)(2,1)S(1)}, u32[]{:S(2)}, u32[]{:S(2)}) collective-permute-start(bf16[33,32,2,512]{3,2,1,0:T(2,128)(2,1)S(1)} %copy-done.9), channel_id=1, source_target_pairs={{0,5},{1,6},{2,7},{3,0},{4,1},{5,2},{6,3},{7,4},{8,13},{9,14},{10,... | collective-permute-start | bytes 6488072 | tf_op jit(solution)/shard_map/ppermute | solution.py:142
  116.2 81.1 %copy-start.8 = (bf16[33,32,2,512]{3,2,1,0:T(2,128)(2,1)S(1)}, bf16[33,32,2,512]{3,2,1,0:T(2,128)(2,1)}, u32[]{:S(2)}) copy-start(bf16[33,32,2,512]{3,2,1,0:T(2,128)(2,1)} %pack_right.11) | copy-start | bytes 6488068
  116.2 81.6 %copy-start.7 = (bf16[33,32,2,512]{3,2,1,0:T(2,128)(2,1)S(1)}, bf16[33,32,2,512]{3,2,1,0:T(2,128)(2,1)}, u32[]{:S(2)}) copy-start(bf16[33,32,2,512]{3,2,1,0:T(2,128)(2,1)} %pack_left.12) | copy-start | bytes 6488068
  197.2 113.8 %collective-permute-start.5 = (bf16[33,32,2,512]{3,2,1,0:T(2,128)(2,1)S(1)}, bf16[33,32,2,512]{3,2,1,0:T(2,128)(2,1)S(1)}, u32[]{:S(2)}, u32[]{:S(2)}) collective-permute-start(bf16[33,32,2,512]{3,2,1,0:T(2,128)(2,1)S(1)} %copy-done.8), channel_id=1, source_target_pairs={{0,24},{8,0},{16,8},{24,16},{1,25},{9,1},{17,9},{25,17},{2,26},{10... | collective-permute-start | bytes 6488072 | tf_op jit(solution)/shard_map/ppermute | solution.py:138
  197.8 121.5 %collective-permute-start.8 = (bf16[33,32,2,512]{3,2,1,0:T(2,128)(2,1)S(1)}, bf16[33,32,2,512]{3,2,1,0:T(2,128)(2,1)S(1)}, u32[]{:S(2)}, u32[]{:S(2)}) collective-permute-start(bf16[33,32,2,512]{3,2,1,0:T(2,128)(2,1)S(1)} %copy-done.7), channel_id=1, source_target_pairs={{0,2},{1,3},{2,4},{3,5},{4,6},{5,7},{6,0},{7,1},{8,10},{9,11},{10,... | collective-permute-start | bytes 6488072 | tf_op jit(solution)/shard_map/ppermute | solution.py:142
  205.1 82.7 %copy-start.6 = (bf16[33,32,2,512]{3,2,1,0:T(2,128)(2,1)S(1)}, bf16[33,32,2,512]{3,2,1,0:T(2,128)(2,1)}, u32[]{:S(2)}) copy-start(bf16[33,32,2,512]{3,2,1,0:T(2,128)(2,1)} %pack_right.12) | copy-start | bytes 6488068
  205.1 83.2 %copy-start.5 = (bf16[33,32,2,512]{3,2,1,0:T(2,128)(2,1)S(1)}, bf16[33,32,2,512]{3,2,1,0:T(2,128)(2,1)}, u32[]{:S(2)}) copy-start(bf16[33,32,2,512]{3,2,1,0:T(2,128)(2,1)} %pack_left.13) | copy-start | bytes 6488068
  287.8 49.1 %collective-permute-start.7 = (bf16[33,32,2,512]{3,2,1,0:T(2,128)(2,1)S(1)}, bf16[33,32,2,512]{3,2,1,0:T(2,128)(2,1)}, u32[]{:S(2)}, u32[]{:S(2)}) collective-permute-start(bf16[33,32,2,512]{3,2,1,0:T(2,128)(2,1)S(1)} %copy-done.6), channel_id=1, source_target_pairs={{0,24},{8,0},{16,8},{24,16},{1,25},{9,1},{17,9},{25,17},{2,26},{10... | collective-permute-start | bytes 6488072 | tf_op jit(solution)/shard_map/ppermute | solution.py:138
  288.3 67.3 %collective-permute-start.10 = (bf16[33,32,2,512]{3,2,1,0:T(2,128)(2,1)S(1)}, bf16[33,32,2,512]{3,2,1,0:T(2,128)(2,1)S(1)}, u32[]{:S(2)}, u32[]{:S(2)}) collective-permute-start(bf16[33,32,2,512]{3,2,1,0:T(2,128)(2,1)S(1)} %copy-done.5), channel_id=1, source_target_pairs={{0,6},{1,7},{2,0},{3,1},{4,2},{5,3},{6,4},{7,5},{8,14},{9,15},{10,... | collective-permute-start | bytes 6488072 | tf_op jit(solution)/shard_map/ppermute | solution.py:142
  307.5 1.6 copy-start.4
  308.0 3.0 copy-start.3
  309.1 66.3 %collective-permute-start.9 = (bf16[33,32,2,512]{3,2,1,0:T(2,128)(2,1)S(1)}, bf16[33,32,2,512]{3,2,1,0:T(2,128)(2,1)}, u32[]{:S(2)}, u32[]{:S(2)}) collective-permute-start(bf16[33,32,2,512]{3,2,1,0:T(2,128)(2,1)S(1)} %copy-done.4), channel_id=1, source_target_pairs={{0,24},{8,0},{16,8},{24,16},{1,25},{9,1},{17,9},{25,17},{2,26},{10... | collective-permute-start | bytes 6488072 | tf_op jit(solution)/shard_map/ppermute | solution.py:138
  311.0 1.4 copy-start.10
  311.0 71.5 %collective-permute-start.12 = (bf16[33,32,2,512]{3,2,1,0:T(2,128)(2,1)S(1)}, bf16[33,32,2,512]{3,2,1,0:T(2,128)(2,1)S(1)}, u32[]{:S(2)}, u32[]{:S(2)}) collective-permute-start(bf16[33,32,2,512]{3,2,1,0:T(2,128)(2,1)S(1)} %copy-done.3), channel_id=1, source_target_pairs={{0,1},{1,2},{2,3},{3,4},{4,5},{5,6},{6,7},{7,0},{8,9},{9,10},{10,1... | collective-permute-start | bytes 6488072 | tf_op jit(solution)/shard_map/ppermute | solution.py:142
  312.4 6.9 %copy-start.2 = (bf16[33,32,2,512]{3,2,1,0:T(2,128)(2,1)S(1)}, bf16[33,32,2,512]{3,2,1,0:T(2,128)(2,1)}, u32[]{:S(2)}) copy-start(bf16[33,32,2,512]{3,2,1,0:T(2,128)(2,1)} %pack_right.14) | copy-start | bytes 6488068
  319.3 17.6 %copy-start.1 = (bf16[33,32,2,512]{3,2,1,0:T(2,128)(2,1)S(1)}, bf16[33,32,2,512]{3,2,1,0:T(2,128)(2,1)}, u32[]{:S(2)}) copy-start(bf16[33,32,2,512]{3,2,1,0:T(2,128)(2,1)} %pack_left.15) | copy-start | bytes 6488068
  319.3 102.4 %collective-permute-start.11 = (bf16[33,32,2,512]{3,2,1,0:T(2,128)(2,1)S(1)}, bf16[33,32,2,512]{3,2,1,0:T(2,128)(2,1)}, u32[]{:S(2)}, u32[]{:S(2)}) collective-permute-start(bf16[33,32,2,512]{3,2,1,0:T(2,128)(2,1)S(1)} %copy-done.2), channel_id=1, source_target_pairs={{0,24},{8,0},{16,8},{24,16},{1,25},{9,1},{17,9},{25,17},{2,26},{10... | collective-permute-start | bytes 6488072 | tf_op jit(solution)/shard_map/ppermute | solution.py:138
  336.9 92.0 %collective-permute-start.14 = (bf16[33,32,2,512]{3,2,1,0:T(2,128)(2,1)S(1)}, bf16[33,32,2,512]{3,2,1,0:T(2,128)(2,1)}, u32[]{:S(2)}, u32[]{:S(2)}) collective-permute-start(bf16[33,32,2,512]{3,2,1,0:T(2,128)(2,1)S(1)} %copy-done.1), channel_id=1, source_target_pairs={{0,7},{1,0},{2,1},{3,2},{4,3},{5,4},{6,5},{7,6},{8,15},{9,8},{10,9... | collective-permute-start | bytes 6488072 | tf_op jit(solution)/shard_map/ppermute | solution.py:142
  348.8 6.9 %copy-start = (bf16[33,32,2,512]{3,2,1,0:T(2,128)(2,1)S(1)}, bf16[33,32,2,512]{3,2,1,0:T(2,128)(2,1)}, u32[]{:S(2)}) copy-start(bf16[33,32,2,512]{3,2,1,0:T(2,128)(2,1)} %pack_right.15) | copy-start | bytes 6488068
  355.7 97.9 %collective-permute-start.13 = (bf16[33,32,2,512]{3,2,1,0:T(2,128)(2,1)S(1)}, bf16[33,32,2,512]{3,2,1,0:T(2,128)(2,1)S(1)}, u32[]{:S(2)}, u32[]{:S(2)}) collective-permute-start(bf16[33,32,2,512]{3,2,1,0:T(2,128)(2,1)S(1)} %copy-done), channel_id=1, source_target_pairs={{0,24},{8,0},{16,8},{24,16},{1,25},{9,1},{17,9},{25,17},{2,26},{10... | collective-permute-start | bytes 6488072 | tf_op jit(solution)/shard_map/ppermute | solution.py:138
  453.6 1.4 copy-start.11
  465.4 2.7 collective-permute-start.15
  468.4 37.0 %collective-permute-start.16 = (f32[2,64,2,512]{3,1,2,0:T(8,128)S(1)}, f32[2,64,2,512]{3,1,2,0:T(8,128)S(1)}, u32[]{:S(2)}, u32[]{:S(2)}) collective-permute-start(f32[2,64,2,512]{3,1,2,0:T(8,128)S(1)} %dynamic-slice_bitcast_fusion), channel_id=1, source_target_pairs={{0,2},{1,3},{2,0},{3,1},{4,6},{5,7},{6,4},{7,5},{8,10},{9,11},{10,... | collective-permute-start | bytes 1572872 | tf_op jit(solution)/shard_map/ppermute | solution.py:81
  505.5 15.1 %collective-permute-start.17 = (f32[1,64,2,512]{3,1,2,0:T(8,128)S(1)}, f32[1,64,2,512]{3,1,2,0:T(8,128)S(1)}, u32[]{:S(2)}, u32[]{:S(2)}) collective-permute-start(f32[1,64,2,512]{3,1,2,0:T(8,128)S(1)} %constant_dynamic-slice_fusion), channel_id=1, source_target_pairs={{0,4},{1,5},{2,6},{3,7},{4,0},{5,1},{6,2},{7,3},{8,12},{9,13},{10,... | collective-permute-start | bytes 786440 | tf_op jit(solution)/shard_map/ppermute | solution.py:81
